TPU v7x, 8 devices: a whole 2x2x1 slice. The times are simulated.
8 devices in a mesh: replica: 1 (over z), tp: 2 (over y), stage: 4 (over x, core).
Axes of the slice: x: 2, y: 2, z: 1, core: 2. Of those that a mesh axis runs over, the one named last changes fastest.
Arguments:
- embeds: bfloat16 [48, 16, 2048], P('replica')
- w_qkv: bfloat16 [4, 2048, 16, 3, 128], P('stage', None, 'tp')
- w_out: bfloat16 [4, 2048, 2048], P('stage', 'tp')
- w_gate: bfloat16 [4, 2048, 5504], P('stage', None, 'tp')
- w_up: bfloat16 [4, 2048, 5504], P('stage', None, 'tp')
- w_down: bfloat16 [4, 5504, 2048], P('stage', 'tp')
- norm_gain: float32 [4, 2, 2048], P('stage')
- k_cache: bfloat16 [4, 48, 16, 16, 16, 128], P('stage', 'replica', None, None, 'tp')
- v_cache: bfloat16 [4, 48, 16, 16, 16, 128], P('stage', 'replica', None, None, 'tp')
- lengths: int32 [48, 16], P('replica')
- final_gain: float32 [2048], replicated
- w_unembed: bfloat16 [2048, 32000], P(None, ('stage', 'tp'))
Outputs:
- output 1: float32 [48, 16, 32000], P('replica', None, ('stage', 'tp'))
- output 2: bfloat16 [4, 48, 16, 16, 16, 128], P('stage', 'replica', None, None, 'tp')
- output 3: bfloat16 [4, 48, 16, 16, 16, 128], P('stage', 'replica', None, None, 'tp')
All inputs are finite; a program needn't handle non-finite values.
Results may differ from a plain program's by a relative error of at most 0.02.
Values are sent between devices in bfloat16 or wider.
A program may use at most 1 GiB of HBM per device.

v0:
```python
import jax
import jax.numpy as jnp
from jax import lax
from jax.sharding import PartitionSpec as P

NORM_EPS = 1e-5
ROPE_THETA = 10000.0


def rms_norm(values, gain_row):
    mean_sq = jnp.mean(values * values, axis=-1, keepdims=True)
    return (values * lax.rsqrt(mean_sq + NORM_EPS) * gain_row).astype(jnp.bfloat16)


def rotate_half(values, cos_part, sin_part):
    half_dim = values.shape[-1] // 2
    first_half = values[..., :half_dim]
    second_half = values[..., half_dim:]
    return jnp.concatenate([first_half * cos_part - second_half * sin_part, second_half * cos_part + first_half * sin_part], axis=-1)


def rope_tables(lengths, head_dim):
    inv_freq = ROPE_THETA ** (-jnp.arange(head_dim // 2, dtype=jnp.float32) * (2.0 / head_dim))
    angles = lengths.astype(jnp.float32)[..., None] * inv_freq
    return jnp.cos(angles), jnp.sin(angles)


def store_group(store_buf, new_rows, group_slot, is_valid, axis_pos):
    kept_rows = lax.dynamic_index_in_dim(store_buf, group_slot, axis_pos, keepdims=False)
    return lax.dynamic_update_index_in_dim(store_buf, jnp.where(is_valid, new_rows, kept_rows), group_slot, axis_pos)


def stage_layers(residual, lengths_row, w_qkv, w_out, w_gate, w_up, w_down, norm_gain, k_group, v_group):
    batch_rows, width = residual.shape
    layer_count = w_qkv.shape[0]
    kv_local = w_qkv.shape[2]
    slot_count = w_qkv.shape[3]
    head_dim = w_qkv.shape[4]
    q_per_kv = slot_count - 2
    cos_part, sin_part = rope_tables(lengths_row, head_dim)
    cos_q = cos_part[:, None, None, :]
    sin_q = sin_part[:, None, None, :]
    cos_k = cos_part[:, None, :]
    sin_k = sin_part[:, None, :]
    visible = (jnp.arange(k_group.shape[2])[None, :] < lengths_row[:, None])[:, None, None, :]
    score_scale = head_dim ** -0.5
    key_rows = []
    val_rows = []
    for layer_idx in range(layer_count):
        normed = rms_norm(residual, norm_gain[layer_idx, 0])
        proj_out = jnp.dot(normed, w_qkv[layer_idx].reshape(width, kv_local * slot_count * head_dim), preferred_element_type=jnp.float32).reshape(batch_rows, kv_local, slot_count, head_dim)
        queries = rotate_half(proj_out[:, :, :q_per_kv], cos_q, sin_q).astype(jnp.bfloat16)
        key_new = rotate_half(proj_out[:, :, q_per_kv], cos_k, sin_k).astype(jnp.bfloat16)
        val_new = proj_out[:, :, q_per_kv + 1].astype(jnp.bfloat16)
        old_scores = jnp.einsum('bkqn,btkn->bkqt', queries, k_group[layer_idx], preferred_element_type=jnp.float32) * score_scale
        old_scores = jnp.where(visible, old_scores, -jnp.inf)
        new_score = jnp.einsum('bkqn,bkn->bkq', queries, key_new, preferred_element_type=jnp.float32) * score_scale
        peak_score = jnp.maximum(jnp.max(old_scores, axis=-1), new_score)
        old_exp = jnp.exp(old_scores - peak_score[..., None])
        new_exp = jnp.exp(new_score - peak_score)
        denom_sum = jnp.sum(old_exp, axis=-1) + new_exp
        old_probs = (old_exp / denom_sum[..., None]).astype(jnp.bfloat16)
        new_probs = (new_exp / denom_sum).astype(jnp.bfloat16)
        attn_out = jnp.einsum('bkqt,btkn->bkqn', old_probs, v_group[layer_idx], preferred_element_type=jnp.float32)
        attn_out = attn_out + jnp.einsum('bkq,bkn->bkqn', new_probs, val_new, preferred_element_type=jnp.float32)
        attn_flat = attn_out.astype(jnp.bfloat16).reshape(batch_rows, kv_local * q_per_kv * head_dim)
        residual = residual + lax.psum(jnp.dot(attn_flat, w_out[layer_idx], preferred_element_type=jnp.float32), 'tp')
        normed_mlp = rms_norm(residual, norm_gain[layer_idx, 1])
        gate_act = jnp.dot(normed_mlp, w_gate[layer_idx], preferred_element_type=jnp.float32)
        up_act = jnp.dot(normed_mlp, w_up[layer_idx], preferred_element_type=jnp.float32)
        hidden = (jax.nn.silu(gate_act) * up_act).astype(jnp.bfloat16)
        residual = residual + lax.psum(jnp.dot(hidden, w_down[layer_idx], preferred_element_type=jnp.float32), 'tp')
        key_rows.append(key_new)
        val_rows.append(val_new)
    return residual, jnp.stack(key_rows), jnp.stack(val_rows)


def solution(mesh):
    stages = mesh.shape['stage']
    cache_spec = P('stage', 'replica', None, None, 'tp', None)
    in_specs = (P('replica'), P('stage', None, 'tp', None, None), P('stage', 'tp', None), P('stage', None, 'tp'), P('stage', None, 'tp'), P('stage', 'tp', None), P('stage'), cache_spec, cache_spec, P('replica'), P(), P(None, ('stage', 'tp')))
    out_specs = (P('replica', None, ('stage', 'tp')), cache_spec, cache_spec)
    next_stage = [(src_idx, src_idx + 1) for src_idx in range(stages - 1)]

    def device_step(embeds, w_qkv, w_out, w_gate, w_up, w_down, norm_gain, k_cache, v_cache, lengths, final_gain, w_unembed):
        group_count, batch_rows, width = embeds.shape
        stage_idx = lax.axis_index('stage')
        row_shape = (k_cache.shape[0], group_count, batch_rows, k_cache.shape[4], k_cache.shape[5])

        def tick_body(tick_idx, loop_state):
            incoming, key_store, val_store, final_rows = loop_state
            group_idx = tick_idx - stage_idx
            is_valid = jnp.logical_and(group_idx >= 0, group_idx < group_count)
            group_slot = jnp.clip(group_idx, 0, group_count - 1)
            first_in = lax.dynamic_index_in_dim(embeds, group_slot, 0, keepdims=False)
            residual = jnp.where(stage_idx == 0, first_in, incoming).astype(jnp.float32)
            lengths_row = lax.dynamic_index_in_dim(lengths, group_slot, 0, keepdims=False)
            k_group = lax.dynamic_index_in_dim(k_cache, group_slot, 1, keepdims=False)
            v_group = lax.dynamic_index_in_dim(v_cache, group_slot, 1, keepdims=False)
            residual, key_rows, val_rows = stage_layers(residual, lengths_row, w_qkv, w_out, w_gate, w_up, w_down, norm_gain, k_group, v_group)
            hidden_out = residual.astype(jnp.bfloat16)
            key_store = store_group(key_store, key_rows, group_slot, is_valid, 1)
            val_store = store_group(val_store, val_rows, group_slot, is_valid, 1)
            final_rows = store_group(final_rows, hidden_out, group_slot, is_valid, 0)
            incoming = lax.ppermute(hidden_out, 'stage', next_stage)
            return incoming, key_store, val_store, final_rows

        start_state = (jnp.zeros((batch_rows, width), jnp.bfloat16), jnp.zeros(row_shape, jnp.bfloat16), jnp.zeros(row_shape, jnp.bfloat16), jnp.zeros((group_count, batch_rows, width), jnp.bfloat16))
        loop_out = lax.fori_loop(0, group_count + stages - 1, tick_body, start_state)
        final_all = lax.psum(jnp.where(stage_idx == stages - 1, loop_out[3], jnp.zeros_like(loop_out[3])), 'stage')
        normed_out = rms_norm(final_all.astype(jnp.float32), final_gain).reshape(group_count * batch_rows, width)
        logits = jnp.dot(normed_out, w_unembed, preferred_element_type=jnp.float32).reshape(group_count, batch_rows, w_unembed.shape[1])
        write_mask = (jnp.arange(k_cache.shape[3])[None, None, :] == lengths[:, :, None])[None, :, :, :, None, None]
        k_out = jnp.where(write_mask, loop_out[1][:, :, :, None], k_cache)
        v_out = jnp.where(write_mask, loop_out[2][:, :, :, None], v_cache)
        return logits, k_out, v_out

    return jax.shard_map(device_step, mesh=mesh, in_specs=in_specs, out_specs=out_specs, check_vma=False)
```

profile of v0, /device:TPU:1, one launch (start us, length us, event | category | flops | bytes accessed | tf_op | source)
XLA Modules:
  0.0 3963.7 jit_solution(18233667124945203381)
XLA Ops:
  8.8 16.4 copy.48
  29.2 3838.3 %while.20 = (s32[]{:T(128)}, bf16[16,2048]{1,0:T(8,128)(2,1)S(1)}, bf16[1,48,16,8,128]{4,2,3,1,0:T(8,128)(2,1)}, bf16[1,48,16,8,128]{4,2,3,1,0:T(8,128)(2,1)S(1)...) while((s32[]{:T(128)}, bf16[16,2048]{1,0:T(8,128)(2,1)S(1)}, ...), condition=%wide.region_7.8_spmd, body=%wide.region_0.7_spmd.sunk | while | flops 812150912 | bytes 59506404 | solution.py:109
  43.5 17.2 all-reduce.6.cloned.1.call-done
  270.5 15.9 all-reduce.6.cloned.1.call-done
  345.8 15.9 all-reduce.6.cloned.1.call-done
  421.0 15.9 all-reduce.6.cloned.1.call-done
  496.2 15.9 all-reduce.6.cloned.1.call-done
  571.5 15.9 all-reduce.6.cloned.1.call-done
  646.7 15.9 all-reduce.6.cloned.1.call-done
  721.9 15.9 all-reduce.6.cloned.1.call-done
  797.2 15.9 all-reduce.6.cloned.1.call-done
  872.4 15.9 all-reduce.6.cloned.1.call-done
  947.6 15.9 all-reduce.6.cloned.1.call-done
  1022.9 15.9 all-reduce.6.cloned.1.call-done
  1098.1 15.9 all-reduce.6.cloned.1.call-done
  1173.3 15.9 all-reduce.6.cloned.1.call-done
  1248.6 15.9 all-reduce.6.cloned.1.call-done
  1323.8 15.9 all-reduce.6.cloned.1.call-done
  1399.0 15.9 all-reduce.6.cloned.1.call-done
  1474.3 15.9 all-reduce.6.cloned.1.call-done
  1549.5 15.9 all-reduce.6.cloned.1.call-done
  1624.7 15.9 all-reduce.6.cloned.1.call-done
  1700.0 15.9 all-reduce.6.cloned.1.call-done
  1775.2 15.9 all-reduce.6.cloned.1.call-done
  1850.4 15.9 all-reduce.6.cloned.1.call-done
  1925.7 15.9 all-reduce.6.cloned.1.call-done
  2000.9 15.9 all-reduce.6.cloned.1.call-done
  2076.1 15.9 all-reduce.6.cloned.1.call-done
  2151.4 15.9 all-reduce.6.cloned.1.call-done
  3871.8 33.6 broadcast_select_fusion
  3905.3 28.2 all-reduce.4.cloned.1.call-done
  3936.1 20.4 fusion.58
  (2183 shorter events, 3411.3 us)
Async XLA Ops:
  43.4 55.2 %all-reduce.8.cloned.1.call-start = ((), (), s32[]{:S(2)}) async-start(), calls=%async_computation.2 | async-start | bytes 262144 | tf_op jit(solution)/shard_map/while/body/eval_jaxpr/psum | solution.py:72
  345.7 53.8 %all-reduce.8.cloned.1.call-start = ((), (), s32[]{:S(2)}) async-start(), calls=%async_computation.2 | async-start | bytes 262144 | tf_op jit(solution)/shard_map/while/body/eval_jaxpr/psum | solution.py:72
  420.9 53.8 %all-reduce.8.cloned.1.call-start = ((), (), s32[]{:S(2)}) async-start(), calls=%async_computation.2 | async-start | bytes 262144 | tf_op jit(solution)/shard_map/while/body/eval_jaxpr/psum | solution.py:72
  496.2 53.8 %all-reduce.8.cloned.1.call-start = ((), (), s32[]{:S(2)}) async-start(), calls=%async_computation.2 | async-start | bytes 262144 | tf_op jit(solution)/shard_map/while/body/eval_jaxpr/psum | solution.py:72
  571.4 53.8 %all-reduce.8.cloned.1.call-start = ((), (), s32[]{:S(2)}) async-start(), calls=%async_computation.2 | async-start | bytes 262144 | tf_op jit(solution)/shard_map/while/body/eval_jaxpr/psum | solution.py:72
  646.6 53.8 %all-reduce.8.cloned.1.call-start = ((), (), s32[]{:S(2)}) async-start(), calls=%async_computation.2 | async-start | bytes 262144 | tf_op jit(solution)/shard_map/while/body/eval_jaxpr/psum | solution.py:72
  721.9 53.8 %all-reduce.8.cloned.1.call-start = ((), (), s32[]{:S(2)}) async-start(), calls=%async_computation.2 | async-start | bytes 262144 | tf_op jit(solution)/shard_map/while/body/eval_jaxpr/psum | solution.py:72
  797.1 53.8 %all-reduce.8.cloned.1.call-start = ((), (), s32[]{:S(2)}) async-start(), calls=%async_computation.2 | async-start | bytes 262144 | tf_op jit(solution)/shard_map/while/body/eval_jaxpr/psum | solution.py:72
  872.3 53.8 %all-reduce.8.cloned.1.call-start = ((), (), s32[]{:S(2)}) async-start(), calls=%async_computation.2 | async-start | bytes 262144 | tf_op jit(solution)/shard_map/while/body/eval_jaxpr/psum | solution.py:72
  947.6 53.8 %all-reduce.8.cloned.1.call-start = ((), (), s32[]{:S(2)}) async-start(), calls=%async_computation.2 | async-start | bytes 262144 | tf_op jit(solution)/shard_map/while/body/eval_jaxpr/psum | solution.py:72
  1022.8 53.8 %all-reduce.8.cloned.1.call-start = ((), (), s32[]{:S(2)}) async-start(), calls=%async_computation.2 | async-start | bytes 262144 | tf_op jit(solution)/shard_map/while/body/eval_jaxpr/psum | solution.py:72
  1098.0 53.8 %all-reduce.8.cloned.1.call-start = ((), (), s32[]{:S(2)}) async-start(), calls=%async_computation.2 | async-start | bytes 262144 | tf_op jit(solution)/shard_map/while/body/eval_jaxpr/psum | solution.py:72
  1173.3 53.8 %all-reduce.8.cloned.1.call-start = ((), (), s32[]{:S(2)}) async-start(), calls=%async_computation.2 | async-start | bytes 262144 | tf_op jit(solution)/shard_map/while/body/eval_jaxpr/psum | solution.py:72
  1248.5 53.8 %all-reduce.8.cloned.1.call-start = ((), (), s32[]{:S(2)}) async-start(), calls=%async_computation.2 | async-start | bytes 262144 | tf_op jit(solution)/shard_map/while/body/eval_jaxpr/psum | solution.py:72
  1323.7 53.8 %all-reduce.8.cloned.1.call-start = ((), (), s32[]{:S(2)}) async-start(), calls=%async_computation.2 | async-start | bytes 262144 | tf_op jit(solution)/shard_map/while/body/eval_jaxpr/psum | solution.py:72
  1399.0 53.8 %all-reduce.8.cloned.1.call-start = ((), (), s32[]{:S(2)}) async-start(), calls=%async_computation.2 | async-start | bytes 262144 | tf_op jit(solution)/shard_map/while/body/eval_jaxpr/psum | solution.py:72
  1474.2 53.8 %all-reduce.8.cloned.1.call-start = ((), (), s32[]{:S(2)}) async-start(), calls=%async_computation.2 | async-start | bytes 262144 | tf_op jit(solution)/shard_map/while/body/eval_jaxpr/psum | solution.py:72
  1549.4 53.8 %all-reduce.8.cloned.1.call-start = ((), (), s32[]{:S(2)}) async-start(), calls=%async_computation.2 | async-start | bytes 262144 | tf_op jit(solution)/shard_map/while/body/eval_jaxpr/psum | solution.py:72
  1624.7 53.8 %all-reduce.8.cloned.1.call-start = ((), (), s32[]{:S(2)}) async-start(), calls=%async_computation.2 | async-start | bytes 262144 | tf_op jit(solution)/shard_map/while/body/eval_jaxpr/psum | solution.py:72
  1775.1 53.8 %all-reduce.8.cloned.1.call-start = ((), (), s32[]{:S(2)}) async-start(), calls=%async_computation.2 | async-start | bytes 262144 | tf_op jit(solution)/shard_map/while/body/eval_jaxpr/psum | solution.py:72
  1850.4 53.8 %all-reduce.8.cloned.1.call-start = ((), (), s32[]{:S(2)}) async-start(), calls=%async_computation.2 | async-start | bytes 262144 | tf_op jit(solution)/shard_map/while/body/eval_jaxpr/psum | solution.py:72
  1925.6 53.8 %all-reduce.8.cloned.1.call-start = ((), (), s32[]{:S(2)}) async-start(), calls=%async_computation.2 | async-start | bytes 262144 | tf_op jit(solution)/shard_map/while/body/eval_jaxpr/psum | solution.py:72
  2000.8 53.8 %all-reduce.8.cloned.1.call-start = ((), (), s32[]{:S(2)}) async-start(), calls=%async_computation.2 | async-start | bytes 262144 | tf_op jit(solution)/shard_map/while/body/eval_jaxpr/psum | solution.py:72
  2076.1 53.8 %all-reduce.8.cloned.1.call-start = ((), (), s32[]{:S(2)}) async-start(), calls=%async_computation.2 | async-start | bytes 262144 | tf_op jit(solution)/shard_map/while/body/eval_jaxpr/psum | solution.py:72
  2151.3 53.8 %all-reduce.8.cloned.1.call-start = ((), (), s32[]{:S(2)}) async-start(), calls=%async_computation.2 | async-start | bytes 262144 | tf_op jit(solution)/shard_map/while/body/eval_jaxpr/psum | solution.py:72
  2226.5 53.8 %all-reduce.8.cloned.1.call-start = ((), (), s32[]{:S(2)}) async-start(), calls=%async_computation.2 | async-start | bytes 262144 | tf_op jit(solution)/shard_map/while/body/eval_jaxpr/psum | solution.py:72
  2301.8 53.8 %all-reduce.8.cloned.1.call-start = ((), (), s32[]{:S(2)}) async-start(), calls=%async_computation.2 | async-start | bytes 262144 | tf_op jit(solution)/shard_map/while/body/eval_jaxpr/psum | solution.py:72
  2377.0 53.8 %all-reduce.8.cloned.1.call-start = ((), (), s32[]{:S(2)}) async-start(), calls=%async_computation.2 | async-start | bytes 262144 | tf_op jit(solution)/shard_map/while/body/eval_jaxpr/psum | solution.py:72
  2452.2 53.8 %all-reduce.8.cloned.1.call-start = ((), (), s32[]{:S(2)}) async-start(), calls=%async_computation.2 | async-start | bytes 262144 | tf_op jit(solution)/shard_map/while/body/eval_jaxpr/psum | solution.py:72
  2527.5 53.8 %all-reduce.8.cloned.1.call-start = ((), (), s32[]{:S(2)}) async-start(), calls=%async_computation.2 | async-start | bytes 262144 | tf_op jit(solution)/shard_map/while/body/eval_jaxpr/psum | solution.py:72
  2602.7 53.8 %all-reduce.8.cloned.1.call-start = ((), (), s32[]{:S(2)}) async-start(), calls=%async_computation.2 | async-start | bytes 262144 | tf_op jit(solution)/shard_map/while/body/eval_jaxpr/psum | solution.py:72
  3867.4 66.1 %all-reduce.4.cloned.1.call-start = ((), (), s32[]{:S(2)}) async-start(), calls=%async_computation | async-start | bytes 6291456 | tf_op jit(solution)/shard_map/psum | solution.py:110
  (175 other events, 4431.5 us)
Sparse Core Ops, SparseCore 0:
  43.5 17.1 all-reduce.5
  270.6 15.7 all-reduce.5
  345.8 15.7 all-reduce.5
  421.1 15.7 all-reduce.5
  496.3 15.7 all-reduce.5
  571.5 15.7 all-reduce.5
  646.8 15.7 all-reduce.5
  722.0 15.7 all-reduce.5
  797.2 15.7 all-reduce.5
  872.5 15.7 all-reduce.5
  947.7 15.7 all-reduce.5
  1022.9 15.7 all-reduce.5
  1098.2 15.7 all-reduce.5
  1173.4 15.7 all-reduce.5
  1248.6 15.7 all-reduce.5
  1323.9 15.7 all-reduce.5
  1399.1 15.7 all-reduce.5
  1474.3 15.7 all-reduce.5
  1549.6 15.7 all-reduce.5
  1624.8 15.7 all-reduce.5
  1700.0 15.7 all-reduce.5
  1775.3 15.7 all-reduce.5
  1850.5 15.7 all-reduce.5
  1925.7 15.7 all-reduce.5
  2001.0 15.7 all-reduce.5
  2076.2 15.7 all-reduce.5
  2151.4 15.7 all-reduce.5
  2226.7 15.7 all-reduce.5
  2301.9 15.7 all-reduce.5
  2377.1 15.7 all-reduce.5
  2452.4 15.7 all-reduce.5
  2527.6 15.7 all-reduce.5
  (70 shorter events, 1099.7 us)
Sparse Core Ops, SparseCore 1:
  3870.8 62.6 all-reduce.3
where the time goes:
time: 3980 us; the launch traced here: 3960 us
  waiting for transfers between devices  1610 us (40%)
  matrix products  1570 us (39%)
  other arithmetic  406 us (10%)
  starting transfers between devices  211 us (5%)
  local copies, waits for them, and re-layouts  140 us (4%)
    psum x51, waiting for transfers between devices, stage_layers(): lax.psum(jnp.dot(attn_flat, w_out[layer_idx], preferred_element_type=jnp....  811 us
    psum x51, waiting for transfers between devices, stage_layers(): lax.psum(jnp.dot(hidden, w_down[layer_idx], preferred_element_type=jnp.fl...  769 us
    dot_general x51, matrix products, stage_layers(): jnp.dot(hidden, w_down[layer_idx], preferred_element_type=jnp.float32)  648 us
    dot_general x51, matrix products, stage_layers(): jnp.dot(normed_mlp, w_gate[layer_idx], preferred_element_type=jnp.float32)  368 us
    dot_general x51, matrix products, stage_layers(): jnp.dot(normed, w_qkv[layer_idx].reshape(width, kv_local * slot_count * h...  323 us
    ppermute x51, starting transfers between devices, tick_body(): incoming = lax.ppermute(hidden_out, 'stage', next_stage)  209 us
    dot_general x51, matrix products, stage_layers(): jnp.dot(attn_flat, w_out[layer_idx], preferred_element_type=jnp.float32)  181 us
    dynamic_update_slice x102, other arithmetic, store_group(): lax.dynamic_update_index_in_dim(store_buf, jnp.where(is_valid, new_rows,...  155 us
  transfers between devices with their start and end apart: 154, of which 103 were waited for; matrix products, arithmetic and copies ran while one was open for 4% of the time, Pallas kernels for 0%

commit v1 on v0

--- a/solution.py
+++ b/solution.py
@@ -23,6 +23,10 @@
     inv_freq = ROPE_THETA ** (-jnp.arange(head_dim // 2, dtype=jnp.float32) * (2.0 / head_dim))
     angles = lengths.astype(jnp.float32)[..., None] * inv_freq
     return jnp.cos(angles), jnp.sin(angles)
+
+
+def tp_sum(partial):
+    return partial + lax.ppermute(partial.astype(jnp.bfloat16), 'tp', [(0, 1), (1, 0)]).astype(jnp.float32)
 
 
 def store_group(store_buf, new_rows, group_slot, is_valid, axis_pos):
@@ -64,12 +68,12 @@
         attn_out = jnp.einsum('bkqt,btkn->bkqn', old_probs, v_group[layer_idx], preferred_element_type=jnp.float32)
         attn_out = attn_out + jnp.einsum('bkq,bkn->bkqn', new_probs, val_new, preferred_element_type=jnp.float32)
         attn_flat = attn_out.astype(jnp.bfloat16).reshape(batch_rows, kv_local * q_per_kv * head_dim)
-        residual = residual + lax.psum(jnp.dot(attn_flat, w_out[layer_idx], preferred_element_type=jnp.float32), 'tp')
+        residual = residual + tp_sum(jnp.dot(attn_flat, w_out[layer_idx], preferred_element_type=jnp.float32))
         normed_mlp = rms_norm(residual, norm_gain[layer_idx, 1])
         gate_act = jnp.dot(normed_mlp, w_gate[layer_idx], preferred_element_type=jnp.float32)
         up_act = jnp.dot(normed_mlp, w_up[layer_idx], preferred_element_type=jnp.float32)
         hidden = (jax.nn.silu(gate_act) * up_act).astype(jnp.bfloat16)
-        residual = residual + lax.psum(jnp.dot(hidden, w_down[layer_idx], preferred_element_type=jnp.float32), 'tp')
+        residual = residual + tp_sum(jnp.dot(hidden, w_down[layer_idx], preferred_element_type=jnp.float32))
         key_rows.append(key_new)
         val_rows.append(val_new)
     return residual, jnp.stack(key_rows), jnp.stack(val_rows)
@@ -83,7 +87,14 @@
     next_stage = [(src_idx, src_idx + 1) for src_idx in range(stages - 1)]
 
     def device_step(embeds, w_qkv, w_out, w_gate, w_up, w_down, norm_gain, k_cache, v_cache, lengths, final_gain, w_unembed):
-        group_count, batch_rows, width = embeds.shape
+        groups, seqs, width = embeds.shape
+        merge = 6
+        group_count, batch_rows = groups // merge, seqs * merge
+        cache_shape = k_cache.shape
+        embeds = embeds.reshape(group_count, batch_rows, width)
+        lengths = lengths.reshape(group_count, batch_rows)
+        k_cache = k_cache.reshape((cache_shape[0], group_count, batch_rows) + cache_shape[3:])
+        v_cache = v_cache.reshape((cache_shape[0], group_count, batch_rows) + cache_shape[3:])
         stage_idx = lax.axis_index('stage')
         row_shape = (k_cache.shape[0], group_count, batch_rows, k_cache.shape[4], k_cache.shape[5])
 
@@ -109,10 +120,10 @@
         loop_out = lax.fori_loop(0, group_count + stages - 1, tick_body, start_state)
         final_all = lax.psum(jnp.where(stage_idx == stages - 1, loop_out[3], jnp.zeros_like(loop_out[3])), 'stage')
         normed_out = rms_norm(final_all.astype(jnp.float32), final_gain).reshape(group_count * batch_rows, width)
-        logits = jnp.dot(normed_out, w_unembed, preferred_element_type=jnp.float32).reshape(group_count, batch_rows, w_unembed.shape[1])
+        logits = jnp.dot(normed_out, w_unembed, preferred_element_type=jnp.float32).reshape(groups, seqs, w_unembed.shape[1])
         write_mask = (jnp.arange(k_cache.shape[3])[None, None, :] == lengths[:, :, None])[None, :, :, :, None, None]
         k_out = jnp.where(write_mask, loop_out[1][:, :, :, None], k_cache)
         v_out = jnp.where(write_mask, loop_out[2][:, :, :, None], v_cache)
-        return logits, k_out, v_out
+        return logits, k_out.reshape(cache_shape), v_out.reshape(cache_shape)
 
     return jax.shard_map(device_step, mesh=mesh, in_specs=in_specs, out_specs=out_specs, check_vma=False)

time: 3980 us -> 923 us (0.23)
  waiting for transfers between devices: 1610 us -> 153 us
  matrix products: 1570 us -> 396 us
  other arithmetic: 406 us -> 98.4 us
  starting transfers between devices: 211 us -> 99.3 us
    psum x102 -> x0, waiting for transfers between devices: 1580 us -> none  [the longest x51 811 us: stage_layers(): lax.psum(jnp.dot(attn_flat, w_out[layer_idx], preferred_element_type=jnp....]
    dot_general x51 -> x11, matrix products: 648 us -> 153 us  [stage_layers(): jnp.dot(hidden, w_down[layer_idx], preferred_element_type=jnp.float32)]
    dot_general x51 -> x11, matrix products: 368 us -> 85.4 us  [stage_layers(): jnp.dot(normed_mlp, w_gate[layer_idx], preferred_element_type=jnp.float32)]
    dot_general x51 -> x11, matrix products: 323 us -> 76.7 us  [stage_layers(): jnp.dot(normed, w_qkv[layer_idx].reshape(width, kv_local * slot_count * h...]
    dot_general x51 -> x11, matrix products: 181 us -> 9.73 us  [stage_layers(): jnp.dot(attn_flat, w_out[layer_idx], preferred_element_type=jnp.float32)]
    ppermute x51 -> x11, starting transfers between devices: 209 us -> 71.1 us  [tick_body(): incoming = lax.ppermute(hidden_out, 'stage', next_stage)]
    dynamic_update_slice x102 -> x11, other arithmetic: 155 us -> 24.3 us  [store_group(): lax.dynamic_update_index_in_dim(store_buf, jnp.where(is_valid, new_rows,...]
    reduce_sum x103 -> x23, other arithmetic: 105 us -> 19.4 us  [rms_norm(): mean_sq = jnp.mean(values * values, axis=-1, keepdims=True)]
  transfers between devices with their start and end apart: 154 -> 34, of which waited for: 103 -> 34; matrix products, arithmetic and copies ran while one was open for 4% -> 9% of each run, Pallas kernels for 0% -> 0%
where the time goes in v1:
time: 923 us; the launch traced here: 918 us
  matrix products  396 us (43%)
  local copies, waits for them, and re-layouts  155 us (17%)
  waiting for transfers between devices  153 us (17%)
  starting transfers between devices  99.3 us (11%)
  other arithmetic  98.4 us (11%)
  between operations  14.1 us (2%)
    dot_general x11, matrix products, stage_layers(): jnp.dot(hidden, w_down[layer_idx], preferred_element_type=jnp.float32)  153 us
    dot_general x11, matrix products, stage_layers(): jnp.dot(normed_mlp, w_gate[layer_idx], preferred_element_type=jnp.float32)  85.4 us
    ppermute x22, waiting for transfers between devices, tp_sum(): lax.ppermute(partial.astype(jnp.bfloat16), 'tp', [(0, 1), (1, 0)])  84.8 us
    dot_general x11, matrix products, stage_layers(): jnp.dot(normed, w_qkv[layer_idx].reshape(width, kv_local * slot_count * h...  76.7 us
    squeeze x11, local copies, waits for them, and re-layouts, stage_layers(): v_group[layer_idx]  71.8 us
    ppermute x11, starting transfers between devices, tick_body(): incoming = lax.ppermute(hidden_out, 'stage', next_stage)  71.1 us
    dynamic_slice x33, local copies, waits for them, and re-layouts, store_group(): lax.dynamic_index_in_dim(store_buf, group_slot, axis_pos, keepdims=False)  40.1 us
    ppermute x11, waiting for transfers between devices, tick_body(): incoming = lax.ppermute(hidden_out, 'stage', next_stage)  39.7 us
  transfers between devices with their start and end apart: 34, of which 34 were waited for; matrix products, arithmetic and copies ran while one was open for 9% of the time, Pallas kernels for 0%

profile of v1, /device:TPU:1, one launch (start us, length us, event | category | flops | bytes accessed | tf_op | source)
XLA Modules:
  0.0 918.4 jit_solution(5388570634629143442)
XLA Ops:
  8.1 16.4 %copy.45 = bf16[1,2048,8,3,128]{1,4,3,2,0:T(8,128)(2,1)} copy(bf16[1,2048,8,3,128]{4,2,3,1,0:T(8,128)(2,1)} %param.15) | data formatting | bytes 25165824 | tf_op jit(solution)/shard_map/while | solution.py:120
  29.3 793.0 %while.20 = (s32[]{:T(128)}, bf16[96,2048]{1,0:T(8,128)(2,1)S(1)}, bf16[1,8,96,8,128]{4,3,2,1,0:T(8,128)(2,1)}, bf16[1,8,96,8,128]{4,3,2,1,0:T(8,128)(2,1)}, bf1...) while((s32[]{:T(128)}, bf16[96,2048]{1,0:T(8,128)(2,1)S(1)}, ...), condition=%wide.region_5.6_spmd, body=%wide.region_0.5_spmd.sunk | while | flops 4873495040 | bytes 113838240 | solution.py:120
  56.0 7.1 collective-permute-done
  63.3 7.8 fusion.117
  71.1 13.9 %fusion.118 = (bf16[96,2048]{1,0:T(8,128)(2,1)}, f32[96,2048]{1,0:T(8,128)}) fusion(bf16[1,2752,2048]{2,1,0:T(8,128)(2,1)} %get-tuple-element.656, bf16[1,2048,2752]{1,2,0:T(8,128)(2,1)} %get-tuple-element.655, f32[96,2752]{1,0:T(8,128)S(1)} %fusion.117, f32[96,2048]{1,0:T(8,128)S(1)} %get-tuple-element.589, f32[2048]{0:T(1024)S(1)} %bitcast.217, ...), kind=kOutput, calls=%fused_computation.101.clone.1 | convolution fusion | flops 2166632448 | bytes 25575808 | tf_op jit(solution)/shard_map/while/body/eval_jaxpr/dot_general | solution.py:76
  136.1 7.8 fusion.117
  143.8 13.9 %fusion.118 = (bf16[96,2048]{1,0:T(8,128)(2,1)}, f32[96,2048]{1,0:T(8,128)}) fusion(bf16[1,2752,2048]{2,1,0:T(8,128)(2,1)} %get-tuple-element.656, bf16[1,2048,2752]{1,2,0:T(8,128)(2,1)} %get-tuple-element.655, f32[96,2752]{1,0:T(8,128)S(1)} %fusion.117, f32[96,2048]{1,0:T(8,128)S(1)} %get-tuple-element.589, f32[2048]{0:T(1024)S(1)} %bitcast.217, ...), kind=kOutput, calls=%fused_computation.101.clone.1 | convolution fusion | flops 2166632448 | bytes 25575808 | tf_op jit(solution)/shard_map/while/body/eval_jaxpr/dot_general | solution.py:76
  179.5 7.0 fusion.104
  207.7 7.8 fusion.117
  215.4 13.9 %fusion.118 = (bf16[96,2048]{1,0:T(8,128)(2,1)}, f32[96,2048]{1,0:T(8,128)}) fusion(bf16[1,2752,2048]{2,1,0:T(8,128)(2,1)} %get-tuple-element.656, bf16[1,2048,2752]{1,2,0:T(8,128)(2,1)} %get-tuple-element.655, f32[96,2752]{1,0:T(8,128)S(1)} %fusion.117, f32[96,2048]{1,0:T(8,128)S(1)} %get-tuple-element.589, f32[2048]{0:T(1024)S(1)} %bitcast.217, ...), kind=kOutput, calls=%fused_computation.101.clone.1 | convolution fusion | flops 2166632448 | bytes 25575808 | tf_op jit(solution)/shard_map/while/body/eval_jaxpr/dot_general | solution.py:76
  251.1 7.0 fusion.104
  279.3 7.8 fusion.117
  287.0 13.9 %fusion.118 = (bf16[96,2048]{1,0:T(8,128)(2,1)}, f32[96,2048]{1,0:T(8,128)}) fusion(bf16[1,2752,2048]{2,1,0:T(8,128)(2,1)} %get-tuple-element.656, bf16[1,2048,2752]{1,2,0:T(8,128)(2,1)} %get-tuple-element.655, f32[96,2752]{1,0:T(8,128)S(1)} %fusion.117, f32[96,2048]{1,0:T(8,128)S(1)} %get-tuple-element.589, f32[2048]{0:T(1024)S(1)} %bitcast.217, ...), kind=kOutput, calls=%fused_computation.101.clone.1 | convolution fusion | flops 2166632448 | bytes 25575808 | tf_op jit(solution)/shard_map/while/body/eval_jaxpr/dot_general | solution.py:76
  322.7 7.0 fusion.104
  350.9 7.8 fusion.117
  358.6 13.9 %fusion.118 = (bf16[96,2048]{1,0:T(8,128)(2,1)}, f32[96,2048]{1,0:T(8,128)}) fusion(bf16[1,2752,2048]{2,1,0:T(8,128)(2,1)} %get-tuple-element.656, bf16[1,2048,2752]{1,2,0:T(8,128)(2,1)} %get-tuple-element.655, f32[96,2752]{1,0:T(8,128)S(1)} %fusion.117, f32[96,2048]{1,0:T(8,128)S(1)} %get-tuple-element.589, f32[2048]{0:T(1024)S(1)} %bitcast.217, ...), kind=kOutput, calls=%fused_computation.101.clone.1 | convolution fusion | flops 2166632448 | bytes 25575808 | tf_op jit(solution)/shard_map/while/body/eval_jaxpr/dot_general | solution.py:76
  394.3 7.0 fusion.104
  422.5 7.8 fusion.117
  430.2 13.9 %fusion.118 = (bf16[96,2048]{1,0:T(8,128)(2,1)}, f32[96,2048]{1,0:T(8,128)}) fusion(bf16[1,2752,2048]{2,1,0:T(8,128)(2,1)} %get-tuple-element.656, bf16[1,2048,2752]{1,2,0:T(8,128)(2,1)} %get-tuple-element.655, f32[96,2752]{1,0:T(8,128)S(1)} %fusion.117, f32[96,2048]{1,0:T(8,128)S(1)} %get-tuple-element.589, f32[2048]{0:T(1024)S(1)} %bitcast.217, ...), kind=kOutput, calls=%fused_computation.101.clone.1 | convolution fusion | flops 2166632448 | bytes 25575808 | tf_op jit(solution)/shard_map/while/body/eval_jaxpr/dot_general | solution.py:76
  494.1 7.8 fusion.117
  501.8 13.9 %fusion.118 = (bf16[96,2048]{1,0:T(8,128)(2,1)}, f32[96,2048]{1,0:T(8,128)}) fusion(bf16[1,2752,2048]{2,1,0:T(8,128)(2,1)} %get-tuple-element.656, bf16[1,2048,2752]{1,2,0:T(8,128)(2,1)} %get-tuple-element.655, f32[96,2752]{1,0:T(8,128)S(1)} %fusion.117, f32[96,2048]{1,0:T(8,128)S(1)} %get-tuple-element.589, f32[2048]{0:T(1024)S(1)} %bitcast.217, ...), kind=kOutput, calls=%fused_computation.101.clone.1 | convolution fusion | flops 2166632448 | bytes 25575808 | tf_op jit(solution)/shard_map/while/body/eval_jaxpr/dot_general | solution.py:76
  565.6 7.8 fusion.117
  573.4 13.9 %fusion.118 = (bf16[96,2048]{1,0:T(8,128)(2,1)}, f32[96,2048]{1,0:T(8,128)}) fusion(bf16[1,2752,2048]{2,1,0:T(8,128)(2,1)} %get-tuple-element.656, bf16[1,2048,2752]{1,2,0:T(8,128)(2,1)} %get-tuple-element.655, f32[96,2752]{1,0:T(8,128)S(1)} %fusion.117, f32[96,2048]{1,0:T(8,128)S(1)} %get-tuple-element.589, f32[2048]{0:T(1024)S(1)} %bitcast.217, ...), kind=kOutput, calls=%fused_computation.101.clone.1 | convolution fusion | flops 2166632448 | bytes 25575808 | tf_op jit(solution)/shard_map/while/body/eval_jaxpr/dot_general | solution.py:76
  637.2 7.8 fusion.117
  645.0 13.9 %fusion.118 = (bf16[96,2048]{1,0:T(8,128)(2,1)}, f32[96,2048]{1,0:T(8,128)}) fusion(bf16[1,2752,2048]{2,1,0:T(8,128)(2,1)} %get-tuple-element.656, bf16[1,2048,2752]{1,2,0:T(8,128)(2,1)} %get-tuple-element.655, f32[96,2752]{1,0:T(8,128)S(1)} %fusion.117, f32[96,2048]{1,0:T(8,128)S(1)} %get-tuple-element.589, f32[2048]{0:T(1024)S(1)} %bitcast.217, ...), kind=kOutput, calls=%fused_computation.101.clone.1 | convolution fusion | flops 2166632448 | bytes 25575808 | tf_op jit(solution)/shard_map/while/body/eval_jaxpr/dot_general | solution.py:76
  708.8 7.8 fusion.117
  716.6 13.9 %fusion.118 = (bf16[96,2048]{1,0:T(8,128)(2,1)}, f32[96,2048]{1,0:T(8,128)}) fusion(bf16[1,2752,2048]{2,1,0:T(8,128)(2,1)} %get-tuple-element.656, bf16[1,2048,2752]{1,2,0:T(8,128)(2,1)} %get-tuple-element.655, f32[96,2752]{1,0:T(8,128)S(1)} %fusion.117, f32[96,2048]{1,0:T(8,128)S(1)} %get-tuple-element.589, f32[2048]{0:T(1024)S(1)} %bitcast.217, ...), kind=kOutput, calls=%fused_computation.101.clone.1 | convolution fusion | flops 2166632448 | bytes 25575808 | tf_op jit(solution)/shard_map/while/body/eval_jaxpr/dot_general | solution.py:76
  780.4 7.8 fusion.117
  788.2 13.9 %fusion.118 = (bf16[96,2048]{1,0:T(8,128)(2,1)}, f32[96,2048]{1,0:T(8,128)}) fusion(bf16[1,2752,2048]{2,1,0:T(8,128)(2,1)} %get-tuple-element.656, bf16[1,2048,2752]{1,2,0:T(8,128)(2,1)} %get-tuple-element.655, f32[96,2752]{1,0:T(8,128)S(1)} %fusion.117, f32[96,2048]{1,0:T(8,128)S(1)} %get-tuple-element.589, f32[2048]{0:T(1024)S(1)} %bitcast.217, ...), kind=kOutput, calls=%fused_computation.101.clone.1 | convolution fusion | flops 2166632448 | bytes 25575808 | tf_op jit(solution)/shard_map/while/body/eval_jaxpr/dot_general | solution.py:76
  826.0 33.5 %broadcast_select_fusion = (bf16[1,48,16,16,8,128]{5,4,3,2,1,0:T(8,128)(2,1)}, bf16[1,48,16,16,8,128]{5,4,3,2,1,0:T(8,128)(2,1)}) fusion(bf16[1,48,16,16,8,128]{5,4,3,2,1,0:T(8,128)(2,1)} %bitcast.210, pred[48,16,16]{2,1,0:T(8,128)(4,1)S(1)} %iota_compare_fusion.1, bf16[48,16,8,128]{3,2,1,0:T(8,128)(2,1)S(1)} %bitcast.213, ...), kind=kLoop, calls=%fused_computation.86 | loop fusion | flops 25165824 | bytes 103821312 | tf_op jit(solution)/shard_map/jit(_where)/select_n | solution.py:126
  859.6 28.8 %all-reduce.2.cloned.1.call-done = bf16[8,96,2048]{2,1,0:T(8,128)(2,1)} async-done(((bf16[8,96,2048]{2,1,0:T(8,128)(2,1)}), bf16[8,96,2048]{2,1,0:T(8,128)(2,1)}) %all-reduce.2.cloned.1.call-update) | async-done | bytes 3145744 | tf_op jit(solution)/shard_map/psum | solution.py:121
  892.0 19.5 %fusion.51 = f32[48,16,4000]{2,1,0:T(8,128)} fusion(bf16[48,16,2048]{2,1,0:T(8,128)(2,1)S(1)} %bitcast.215, bf16[2048,4000]{0,1:T(8,128)(2,1)} %param.25), kind=kOutput, calls=%fused_computation.88 | convolution fusion | flops 12582912000 | bytes 31817728 | tf_op jit(solution)/shard_map/dot_general | solution.py:123
  (480 shorter events, 530.7 us)
Async XLA Ops:
  7.2 881.2 %all-reduce.2.cloned.1.call-start = ((), (), s32[]{:S(2)}) async-start(), calls=%async_computation | async-start | bytes 6291456 | tf_op jit(solution)/shard_map/psum | solution.py:121
  52.1 10.9 %collective-permute-start = (bf16[96,2048]{1,0:T(8,128)(2,1)S(1)}, bf16[96,2048]{1,0:T(8,128)(2,1)S(1)}, u32[]{:S(2)}, u32[]{:S(2)}) collective-permute-start(bf16[96,2048]{1,0:T(8,128)(2,1)S(1)} %get-tuple-element.588), channel_id=1, source_target_pairs={{0,4},{4,0},{1,5},{5,1},{2,6},{6,2},{3,7},{7,3}} | collective-permute-start | bytes 1179656 | tf_op jit(solution)/shard_map/while/body/eval_jaxpr/ppermute | solution.py:29
  85.0 9.4 %collective-permute-start.1 = (bf16[96,2048]{1,0:T(8,128)(2,1)}, bf16[96,2048]{1,0:T(8,128)(2,1)S(1)}, u32[]{:S(2)}, u32[]{:S(2)}) collective-permute-start(bf16[96,2048]{1,0:T(8,128)(2,1)} %get-tuple-element.593), channel_id=1, source_target_pairs={{0,4},{4,0},{1,5},{5,1},{2,6},{6,2},{3,7},{7,3}} | collective-permute-start | bytes 1179656 | tf_op jit(solution)/shard_map/while/body/eval_jaxpr/ppermute | solution.py:29
  96.6 9.7 %collective-permute-start.2 = (bf16[96,2048]{1,0:T(8,128)(2,1)S(1)}, bf16[96,2048]{1,0:T(8,128)(2,1)S(1)}, u32[]{:S(2)}, u32[]{:S(2)}) collective-permute-start(bf16[96,2048]{1,0:T(8,128)(2,1)S(1)} %get-tuple-element.594), channel_id=1, source_target_pairs={{0,1},{1,2},{2,3},{4,5},{5,6},{6,7}} | collective-permute-start | bytes 1179656 | tf_op jit(solution)/shard_map/while/body/eval_jaxpr/ppermute | solution.py:116
  129.1 6.6 collective-permute-start
  157.7 7.4 collective-permute-start.1
  167.4 10.6 %collective-permute-start.2 = (bf16[96,2048]{1,0:T(8,128)(2,1)S(1)}, bf16[96,2048]{1,0:T(8,128)(2,1)S(1)}, u32[]{:S(2)}, u32[]{:S(2)}) collective-permute-start(bf16[96,2048]{1,0:T(8,128)(2,1)S(1)} %get-tuple-element.594), channel_id=1, source_target_pairs={{0,1},{1,2},{2,3},{4,5},{5,6},{6,7}} | collective-permute-start | bytes 1179656 | tf_op jit(solution)/shard_map/while/body/eval_jaxpr/ppermute | solution.py:116
  200.7 6.6 collective-permute-start
  229.3 6.6 collective-permute-start.1
  238.2 11.4 %collective-permute-start.2 = (bf16[96,2048]{1,0:T(8,128)(2,1)S(1)}, bf16[96,2048]{1,0:T(8,128)(2,1)S(1)}, u32[]{:S(2)}, u32[]{:S(2)}) collective-permute-start(bf16[96,2048]{1,0:T(8,128)(2,1)S(1)} %get-tuple-element.594), channel_id=1, source_target_pairs={{0,1},{1,2},{2,3},{4,5},{5,6},{6,7}} | collective-permute-start | bytes 1179656 | tf_op jit(solution)/shard_map/while/body/eval_jaxpr/ppermute | solution.py:116
  272.3 6.6 collective-permute-start
  300.9 6.6 collective-permute-start.1
  309.8 11.4 %collective-permute-start.2 = (bf16[96,2048]{1,0:T(8,128)(2,1)S(1)}, bf16[96,2048]{1,0:T(8,128)(2,1)S(1)}, u32[]{:S(2)}, u32[]{:S(2)}) collective-permute-start(bf16[96,2048]{1,0:T(8,128)(2,1)S(1)} %get-tuple-element.594), channel_id=1, source_target_pairs={{0,1},{1,2},{2,3},{4,5},{5,6},{6,7}} | collective-permute-start | bytes 1179656 | tf_op jit(solution)/shard_map/while/body/eval_jaxpr/ppermute | solution.py:116
  343.9 6.6 collective-permute-start
  372.5 6.6 collective-permute-start.1
  381.3 11.4 %collective-permute-start.2 = (bf16[96,2048]{1,0:T(8,128)(2,1)S(1)}, bf16[96,2048]{1,0:T(8,128)(2,1)S(1)}, u32[]{:S(2)}, u32[]{:S(2)}) collective-permute-start(bf16[96,2048]{1,0:T(8,128)(2,1)S(1)} %get-tuple-element.594), channel_id=1, source_target_pairs={{0,1},{1,2},{2,3},{4,5},{5,6},{6,7}} | collective-permute-start | bytes 1179656 | tf_op jit(solution)/shard_map/while/body/eval_jaxpr/ppermute | solution.py:116
  415.5 6.6 collective-permute-start
  444.1 6.6 collective-permute-start.1
  452.9 11.4 %collective-permute-start.2 = (bf16[96,2048]{1,0:T(8,128)(2,1)S(1)}, bf16[96,2048]{1,0:T(8,128)(2,1)S(1)}, u32[]{:S(2)}, u32[]{:S(2)}) collective-permute-start(bf16[96,2048]{1,0:T(8,128)(2,1)S(1)} %get-tuple-element.594), channel_id=1, source_target_pairs={{0,1},{1,2},{2,3},{4,5},{5,6},{6,7}} | collective-permute-start | bytes 1179656 | tf_op jit(solution)/shard_map/while/body/eval_jaxpr/ppermute | solution.py:116
  487.1 6.6 collective-permute-start
  515.7 6.6 collective-permute-start.1
  524.5 11.4 %collective-permute-start.2 = (bf16[96,2048]{1,0:T(8,128)(2,1)S(1)}, bf16[96,2048]{1,0:T(8,128)(2,1)S(1)}, u32[]{:S(2)}, u32[]{:S(2)}) collective-permute-start(bf16[96,2048]{1,0:T(8,128)(2,1)S(1)} %get-tuple-element.594), channel_id=1, source_target_pairs={{0,1},{1,2},{2,3},{4,5},{5,6},{6,7}} | collective-permute-start | bytes 1179656 | tf_op jit(solution)/shard_map/while/body/eval_jaxpr/ppermute | solution.py:116
  558.7 6.6 collective-permute-start
  596.1 11.4 %collective-permute-start.2 = (bf16[96,2048]{1,0:T(8,128)(2,1)S(1)}, bf16[96,2048]{1,0:T(8,128)(2,1)S(1)}, u32[]{:S(2)}, u32[]{:S(2)}) collective-permute-start(bf16[96,2048]{1,0:T(8,128)(2,1)S(1)} %get-tuple-element.594), channel_id=1, source_target_pairs={{0,1},{1,2},{2,3},{4,5},{5,6},{6,7}} | collective-permute-start | bytes 1179656 | tf_op jit(solution)/shard_map/while/body/eval_jaxpr/ppermute | solution.py:116
  630.3 6.6 collective-permute-start
  658.9 6.6 collective-permute-start.1
  667.7 11.4 %collective-permute-start.2 = (bf16[96,2048]{1,0:T(8,128)(2,1)S(1)}, bf16[96,2048]{1,0:T(8,128)(2,1)S(1)}, u32[]{:S(2)}, u32[]{:S(2)}) collective-permute-start(bf16[96,2048]{1,0:T(8,128)(2,1)S(1)} %get-tuple-element.594), channel_id=1, source_target_pairs={{0,1},{1,2},{2,3},{4,5},{5,6},{6,7}} | collective-permute-start | bytes 1179656 | tf_op jit(solution)/shard_map/while/body/eval_jaxpr/ppermute | solution.py:116
  701.9 6.6 collective-permute-start
  739.3 11.4 %collective-permute-start.2 = (bf16[96,2048]{1,0:T(8,128)(2,1)S(1)}, bf16[96,2048]{1,0:T(8,128)(2,1)S(1)}, u32[]{:S(2)}, u32[]{:S(2)}) collective-permute-start(bf16[96,2048]{1,0:T(8,128)(2,1)S(1)} %get-tuple-element.594), channel_id=1, source_target_pairs={{0,1},{1,2},{2,3},{4,5},{5,6},{6,7}} | collective-permute-start | bytes 1179656 | tf_op jit(solution)/shard_map/while/body/eval_jaxpr/ppermute | solution.py:116
  773.5 6.6 collective-permute-start
  802.1 6.6 collective-permute-start.1
  810.9 11.4 %collective-permute-start.2 = (bf16[96,2048]{1,0:T(8,128)(2,1)S(1)}, bf16[96,2048]{1,0:T(8,128)(2,1)S(1)}, u32[]{:S(2)}, u32[]{:S(2)}) collective-permute-start(bf16[96,2048]{1,0:T(8,128)(2,1)S(1)} %get-tuple-element.594), channel_id=1, source_target_pairs={{0,1},{1,2},{2,3},{4,5},{5,6},{6,7}} | collective-permute-start | bytes 1179656 | tf_op jit(solution)/shard_map/while/body/eval_jaxpr/ppermute | solution.py:116
  (18 other events, 90.2 us)
Sparse Core Ops, SparseCore 0:
  824.3 64.0 all-reduce.1

commit v2 on v0

v2 whole, which is shorter than its diff:
```python
import functools

import jax
import jax.numpy as jnp
from jax import lax
from jax.experimental import pallas as pl
from jax.experimental.pallas import tpu as pltpu
from jax.sharding import PartitionSpec as P

NORM_EPS = 1e-5
ROPE_THETA = 10000.0
MESH = pl.DeviceIdType.MESH
F32 = jnp.float32
BF16 = jnp.bfloat16
MERGE = 3
TAIL_ROWS = 48
VMEM_LIMIT = 67043328


def rms_norm(values, gain_row):
    mean_sq = jnp.mean(values * values, axis=-1, keepdims=True)
    return (values * lax.rsqrt(mean_sq + NORM_EPS) * gain_row).astype(BF16)


def rope_tables(lengths, head_dim):
    inv_freq = ROPE_THETA ** (-jnp.arange(head_dim // 2, dtype=F32) * (2.0 / head_dim))
    angles = lengths.astype(F32)[..., None] * inv_freq
    cos_part, sin_part = jnp.cos(angles), jnp.sin(angles)
    return jnp.concatenate([cos_part, cos_part], -1), jnp.concatenate([-sin_part, sin_part], -1)


def column_chunks(total, width):
    return [(low, min(width, total - low)) for low in range(0, total, width)]


def dot(lhs, rhs):
    return jnp.dot(lhs, rhs, preferred_element_type=F32)


def pipeline_kernel(
    stages, batch, lens_ref, gain_ref, cos_ref, sin_ref, emb_ref, wqkv_hbm, wout_hbm, wgate_hbm, wup_hbm, wdown_hbm, kc_hbm, vc_hbm,
    final_ref, knew_ref, vnew_ref,
    wqkv, wout, wgate, wup, wdown, kbuf, vbuf, xbuf, xout, resid, send_a, recv_a, send_d, recv_d, unit, hidden, attn, q_scr, k_scr, v_scr, o_scr,
    w_sem, c_sem, n_sem, e_sem, a_send, a_recv, d_send, d_recv, x_send, x_recv, f_send, f_recv, credit,
):
    stage = lax.axis_index("stage")
    peer = {"tp": 1 - lax.axis_index("tp")}
    last = stages - 1
    rows = emb_ref.shape[0]
    count = rows // batch
    heads, head_dim = kbuf.shape[2], kbuf.shape[3]
    slots = kbuf.shape[1]
    scale = head_dim ** -0.5
    weights = [pltpu.make_async_copy(src, dst, w_sem.at[i]) for i, (src, dst) in enumerate(
        [(wqkv_hbm, wqkv), (wout_hbm, wout), (wgate_hbm, wgate), (wup_hbm, wup), (wdown_hbm, wdown)])]

    def span(step):
        return pl.ds(pl.multiple_of(step * batch, batch), batch)

    def emb_copy(step):
        return pltpu.make_async_copy(emb_ref.at[span(step)], xbuf.at[lax.rem(step, 2)], e_sem.at[lax.rem(step, 2)])

    def cache_copies(step):
        return (pltpu.make_async_copy(kc_hbm.at[span(step)], kbuf, c_sem.at[0]), pltpu.make_async_copy(vc_hbm.at[span(step)], vbuf, c_sem.at[1]))

    def new_copies(step):
        return (pltpu.make_async_copy(k_scr, knew_ref.at[span(step)], n_sem.at[0]), pltpu.make_async_copy(v_scr, vnew_ref.at[span(step)], n_sem.at[1]))

    def sum_copy(step, send, recv, send_sem, recv_sem):
        slot = lax.rem(step, 2)
        return pltpu.make_async_remote_copy(send.at[slot], recv.at[slot], send_sem.at[slot], recv_sem.at[slot], device_id=peer, device_id_type=MESH)

    def hop_copy(step):
        slot = lax.rem(step, 2)
        return pltpu.make_async_remote_copy(xout.at[slot], xbuf.at[slot], x_send.at[slot], x_recv.at[slot], device_id={"stage": stage + 1}, device_id_type=MESH)

    def final_copies(step):
        slot = lax.rem(step, 2)
        return [pltpu.make_async_remote_copy(xout.at[slot], final_ref.at[span(step)], f_send.at[slot, dst], f_recv.at[step], device_id={"stage": dst}, device_id_type=MESH)
                for dst in range(last)]

    def final_local(step):
        slot = lax.rem(step, 2)
        return pltpu.make_async_copy(xout.at[slot], final_ref.at[span(step)], f_send.at[slot, last])

    for copy in weights[:1] + list(cache_copies(0)) + weights[1:]:
        copy.start()

    @pl.when(stage == 0)
    def _():
        emb_copy(0).start()
        emb_copy(1).start()

    def attend(step):
        slot = lax.rem(step, 2)

        @pl.when(stage == 0)
        def _():
            emb_copy(step).wait()

        @pl.when(stage > 0)
        def _():
            pltpu.make_async_remote_copy(xout.at[slot], xbuf.at[slot], x_send.at[slot], x_recv.at[slot], device_id={"stage": stage}, device_id_type=MESH).wait_recv()

        @pl.when(step == 0)
        def _():
            weights[0].wait()

        @pl.when(step > 0)
        def _():
            for copy in new_copies(step - 1):
                copy.wait()

        unit[...] = rms_norm(xbuf[slot].astype(F32), gain_ref[0:1, :])
        cos_part = cos_ref[span(step), :]
        sin_part = sin_ref[span(step), :]
        for low, width in column_chunks(wqkv.shape[1], 6 * head_dim):
            proj = dot(unit[...], wqkv[:, low:low + width])
            for part in range(width // (3 * head_dim)):
                head = low // (3 * head_dim) + part
                base = part * 3 * head_dim
                query = proj[:, base:base + head_dim]
                key = proj[:, base + head_dim:base + 2 * head_dim]
                q_scr[:, head, :] = (query * cos_part + pltpu.roll(query, head_dim // 2, 1) * sin_part).astype(BF16).astype(F32)
                k_scr[:, head, :] = (key * cos_part + pltpu.roll(key, head_dim // 2, 1) * sin_part).astype(BF16).astype(F32)
                v_scr[:, head, :] = proj[:, base + 2 * head_dim:base + 3 * head_dim].astype(BF16).astype(F32)
        for copy in cache_copies(step):
            copy.wait()
        for copy in new_copies(step):
            copy.start()
        position = lax.broadcasted_iota(jnp.int32, (slots, heads, 1), 0)

        def one_row(row):
            length = lens_ref[step * batch + row]
            query = q_scr[row]
            scores = jnp.sum(query[None] * kbuf[row].astype(F32), axis=-1, keepdims=True) * scale
            scores = jnp.where(position < length, scores, -jnp.inf)
            fresh = jnp.sum(query * k_scr[row], axis=-1, keepdims=True) * scale
            peak = jnp.maximum(jnp.max(scores, axis=0), fresh)
            exps = jnp.exp(scores - peak[None])
            fresh_exp = jnp.exp(fresh - peak)
            inverse = 1.0 / (jnp.sum(exps, axis=0) + fresh_exp)
            probs = (exps * inverse[None]).astype(BF16).astype(F32)
            fresh_prob = (fresh_exp * inverse).astype(BF16).astype(F32)
            o_scr[row] = jnp.sum(probs * vbuf[row].astype(F32), axis=0) + fresh_prob * v_scr[row]

        def rows_body(index, carry):
            for sub in range(2):
                one_row(index * 2 + sub)
            return carry

        lax.fori_loop(0, batch // 2, rows_body, 0)

        @pl.when(step + 1 < count)
        def _():
            for copy in cache_copies(step + 1):
                copy.start()

    def project(step):
        slot = lax.rem(step, 2)

        @pl.when(step == 0)
        def _():
            weights[1].wait()

        for head in range(heads):
            attn[:, head * head_dim:(head + 1) * head_dim] = o_scr[:, head, :].astype(BF16)
        for low, width in column_chunks(wout.shape[1], 1024):
            partial = dot(attn[...], wout[:, low:low + width])
            send_a[slot, :, low:low + width] = partial.astype(BF16)
            resid[slot, :, low:low + width] = xbuf[slot, :, low:low + width].astype(F32) + partial
        sum_copy(step, send_a, recv_a, a_send, a_recv).start()

        @pl.when(jnp.logical_and(stage == 0, step + 2 < count))
        def _():
            emb_copy(step + 2).start()

        @pl.when(jnp.logical_and(stage > 0, step + 2 < count))
        def _():
            pl.semaphore_signal(credit, inc=1, device_id={"stage": stage - 1}, device_id_type=MESH)

    def feed_forward(step):
        slot = lax.rem(step, 2)

        @pl.when(step == 0)
        def _():
            for copy in weights[2:]:
                copy.wait()

        sum_copy(step, send_a, recv_a, a_send, a_recv).wait()
        summed = resid[slot] + recv_a[slot].astype(F32)
        resid[slot] = summed
        unit[...] = rms_norm(summed, gain_ref[1:2, :])
        for low, width in column_chunks(wgate.shape[1], 768):
            gate = dot(unit[...], wgate[:, low:low + width])
            up = dot(unit[...], wup[:, low:low + width])
            hidden[:, low:low + width] = (jax.nn.silu(gate) * up).astype(BF16)
        for low, width in column_chunks(wdown.shape[1], 1024):
            partial = dot(hidden[...], wdown[:, low:low + width])
            send_d[slot, :, low:low + width] = partial.astype(BF16)
            resid[slot, :, low:low + width] = resid[slot, :, low:low + width] + partial
        sum_copy(step, send_d, recv_d, d_send, d_recv).start()

    def hand_on(step):
        slot = lax.rem(step, 2)
        sum_copy(step, send_d, recv_d, d_send, d_recv).wait()

        @pl.when(jnp.logical_and(stage < last, step >= 2))
        def _():
            hop_copy(step - 2).wait_send()
            pl.semaphore_wait(credit, 1)

        @pl.when(jnp.logical_and(stage == last, step >= 2))
        def _():
            for copy in final_copies(step - 2):
                copy.wait_send()
            final_local(step - 2).wait()

        xout[slot] = (resid[slot] + recv_d[slot].astype(F32)).astype(BF16)

        @pl.when(stage < last)
        def _():
            hop_copy(step).start()

        @pl.when(stage == last)
        def _():
            for copy in final_copies(step):
                copy.start()
            final_local(step).start()

    def slot_body(step, carry):
        @pl.when(step < count)
        def _():
            attend(step)

        @pl.when(step >= 2)
        def _():
            hand_on(step - 2)

        @pl.when(step < count)
        def _():
            project(step)

        @pl.when(jnp.logical_and(step >= 1, step <= count))
        def _():
            feed_forward(step - 1)

        return carry

    lax.fori_loop(0, count + 2, slot_body, 0)
    for copy in new_copies(count - 1):
        copy.wait()

    @pl.when(stage < last)
    def _():
        for step in (count - 2, count - 1):
            hop_copy(step).wait_send()

        def drain(step, carry):
            pltpu.make_async_remote_copy(xout.at[0], final_ref.at[span(step)], f_send.at[0, 0], f_recv.at[step], device_id={"stage": stage}, device_id_type=MESH).wait_recv()
            return carry

        lax.fori_loop(0, count, drain, 0)

    @pl.when(stage == last)
    def _():
        for step in (count - 2, count - 1):
            for copy in final_copies(step):
                copy.wait_send()
            final_local(step).wait()


def run_pipeline(stages, lens, gains, cos_part, sin_part, embeds, wqkv, wout, wgate, wup, wdown, k_cache, v_cache):
    rows, width = embeds.shape
    batch = 16 * MERGE
    slots, heads, head_dim = k_cache.shape[1:]
    count = rows // batch
    anywhere = pl.BlockSpec(memory_space=pl.ANY)
    local = pl.BlockSpec(memory_space=pltpu.VMEM)
    pair = pltpu.SemaphoreType.DMA((2,))
    new_rows = jax.ShapeDtypeStruct((rows, heads, head_dim), F32)
    return pl.pallas_call(
        functools.partial(pipeline_kernel, stages, batch),
        out_shape=(jax.ShapeDtypeStruct((rows, width), BF16), new_rows, new_rows),
        in_specs=[pl.BlockSpec(memory_space=pltpu.SMEM), local, local, local] + [anywhere] * 8,
        out_specs=(anywhere, anywhere, anywhere),
        scratch_shapes=[
            pltpu.VMEM(wqkv.shape, BF16), pltpu.VMEM(wout.shape, BF16), pltpu.VMEM(wgate.shape, BF16), pltpu.VMEM(wup.shape, BF16), pltpu.VMEM(wdown.shape, BF16),
            pltpu.VMEM((batch, slots, heads, head_dim), BF16), pltpu.VMEM((batch, slots, heads, head_dim), BF16),
            pltpu.VMEM((2, batch, width), BF16), pltpu.VMEM((2, batch, width), BF16), pltpu.VMEM((2, batch, width), F32),
            pltpu.VMEM((2, batch, width), BF16), pltpu.VMEM((2, batch, width), BF16), pltpu.VMEM((2, batch, width), BF16), pltpu.VMEM((2, batch, width), BF16),
            pltpu.VMEM((batch, width), BF16), pltpu.VMEM((batch, wgate.shape[1]), BF16), pltpu.VMEM((batch, heads * head_dim), BF16),
            pltpu.VMEM((batch, heads, head_dim), F32), pltpu.VMEM((batch, heads, head_dim), F32), pltpu.VMEM((batch, heads, head_dim), F32), pltpu.VMEM((batch, heads, head_dim), F32),
            pltpu.SemaphoreType.DMA((5,)), pair, pair, pair, pair, pair, pair, pair, pair, pair,
            pltpu.SemaphoreType.DMA((2, stages)), pltpu.SemaphoreType.DMA((count,)), pltpu.SemaphoreType.REGULAR,
        ],
        compiler_params=pltpu.CompilerParams(has_side_effects=True, vmem_limit_bytes=VMEM_LIMIT),
    )(lens, gains, cos_part, sin_part, embeds, wqkv, wout, wgate, wup, wdown, k_cache, v_cache)


def tail_kernel(lens_ref, gain_ref, final_ref, knew_ref, vnew_ref, kc_ref, vc_ref, wun_ref, logits_ref, ko_ref, vo_ref):
    block = pl.program_id(0)
    rows = kc_ref.shape[0]
    ko_ref[...] = kc_ref[...]
    vo_ref[...] = vc_ref[...]

    def place(row, carry):
        length = lens_ref[block * rows + row]
        ko_ref[row, length] = knew_ref[row].astype(BF16)
        vo_ref[row, length] = vnew_ref[row].astype(BF16)
        return carry

    lax.fori_loop(0, rows, place, 0)
    normed = rms_norm(final_ref[...].astype(F32), gain_ref[...])
    for low, width in column_chunks(wun_ref.shape[1], 1024):
        logits_ref[:, low:low + width] = dot(normed, wun_ref[:, low:low + width])


def run_tail(lens, gain, final, knew, vnew, k_cache, v_cache, wun):
    rows, width = final.shape
    slots, heads, head_dim = k_cache.shape[1:]
    vocab = wun.shape[1]
    cache_spec = pl.BlockSpec((TAIL_ROWS, slots, heads, head_dim), lambda i, lens: (i, 0, 0, 0))
    new_spec = pl.BlockSpec((TAIL_ROWS, heads, head_dim), lambda i, lens: (i, 0, 0))
    return pl.pallas_call(
        tail_kernel,
        out_shape=(jax.ShapeDtypeStruct((rows, vocab), F32), jax.ShapeDtypeStruct(k_cache.shape, BF16), jax.ShapeDtypeStruct(v_cache.shape, BF16)),
        grid_spec=pltpu.PrefetchScalarGridSpec(
            num_scalar_prefetch=1,
            grid=(rows // TAIL_ROWS,),
            in_specs=[pl.BlockSpec((1, width), lambda i, lens: (0, 0)), pl.BlockSpec((TAIL_ROWS, width), lambda i, lens: (i, 0)), new_spec, new_spec, cache_spec, cache_spec,
                      pl.BlockSpec((width, vocab), lambda i, lens: (0, 0), pipeline_mode=pl.Buffered(1))],
            out_specs=(pl.BlockSpec((TAIL_ROWS, vocab), lambda i, lens: (i, 0)), cache_spec, cache_spec),
        ),
        compiler_params=pltpu.CompilerParams(dimension_semantics=("arbitrary",), vmem_limit_bytes=VMEM_LIMIT),
    )(lens, gain, final, knew, vnew, k_cache, v_cache, wun)


def solution(mesh):
    stages = mesh.shape['stage']
    cache_spec = P('stage', 'replica', None, None, 'tp', None)
    in_specs = (P('replica'), P('stage', None, 'tp', None, None), P('stage', 'tp', None), P('stage', None, 'tp'), P('stage', None, 'tp'), P('stage', 'tp', None), P('stage'), cache_spec, cache_spec, P('replica'), P(), P(None, ('stage', 'tp')))
    out_specs = (P('replica', None, ('stage', 'tp')), cache_spec, cache_spec)

    def device_step(embeds, w_qkv, w_out, w_gate, w_up, w_down, norm_gain, k_cache, v_cache, lengths, final_gain, w_unembed):
        groups, seqs, width = embeds.shape
        rows = groups * seqs
        cache_shape = k_cache.shape
        head_dim = cache_shape[-1]
        lens = lengths.reshape(rows)
        cos_part, sin_part = rope_tables(lens, head_dim)
        k_rows = k_cache.reshape((rows,) + cache_shape[3:])
        v_rows = v_cache.reshape((rows,) + cache_shape[3:])
        final, knew, vnew = run_pipeline(
            stages, lens, norm_gain[0], cos_part, sin_part, embeds.reshape(rows, width), w_qkv[0].reshape(width, -1), w_out[0], w_gate[0], w_up[0], w_down[0], k_rows, v_rows)
        logits, k_out, v_out = run_tail(lens, final_gain.reshape(1, width), final, knew, vnew, k_rows, v_rows, w_unembed)
        return logits.reshape(groups, seqs, -1), k_out.reshape(cache_shape), v_out.reshape(cache_shape)

    return jax.shard_map(device_step, mesh=mesh, in_specs=in_specs, out_specs=out_specs, check_vma=False)
```

time: 3980 us -> 535 us (0.13)
  waiting for transfers between devices: 1610 us -> 0 us
  matrix products: 1570 us -> 0 us
  Pallas kernels: 0 us -> 443 us
  other arithmetic: 406 us -> 2.61 us
  starting transfers between devices: 211 us -> 0 us
  local copies, waits for them, and re-layouts: 140 us -> 86.5 us
    psum x103 -> x0, waiting for transfers between devices: 1610 us -> none  [the longest x51 811 us: stage_layers(): lax.psum(jnp.dot(attn_flat, w_out[layer_idx], preferred_element_type=jnp....]
    dot_general x307 -> x0, matrix products: 1570 us -> none  [the longest x51 648 us: stage_layers(): jnp.dot(hidden, w_down[layer_idx], preferred_element_type=jnp.float32)]
    pallas_call x0 -> x2, Pallas kernels: none -> 443 us  [the longest x1 374 us: run_pipeline(): pl.pallas_call(functools.partial(pipeline_kernel, stages, batch), out_sha...]
    ppermute x51 -> x0, starting transfers between devices: 209 us -> none  [tick_body(): incoming = lax.ppermute(hidden_out, 'stage', next_stage)]
    dynamic_update_slice x102 -> x0, other arithmetic: 155 us -> none  [store_group(): lax.dynamic_update_index_in_dim(store_buf, jnp.where(is_valid, new_rows,...]
    reduce_sum x154 -> x0, other arithmetic: 114 us -> none  [the longest x103 105 us: rms_norm(): mean_sq = jnp.mean(values * values, axis=-1, keepdims=True)]
    unnamed x4 -> x7, local copies, waits for them, and re-layouts: 0.01 us -> 69.8 us
    squeeze x102 -> x0, local copies, waits for them, and re-layouts: 65.1 us -> none  [the longest x51 64.8 us: stage_layers(): v_group[layer_idx]]
  transfers between devices with their start and end apart: 154 -> 0, of which waited for: 103 -> 0; matrix products, arithmetic and copies ran while one was open for 4% -> 0% of each run, Pallas kernels for 0% -> 0%
where the time goes in v2:
time: 535 us; the launch traced here: 533 us
  Pallas kernels  443 us (83%)
  local copies, waits for them, and re-layouts  86.5 us (16%)
    pallas_call x1, Pallas kernels, run_pipeline(): pl.pallas_call(functools.partial(pipeline_kernel, stages, batch), out_sha...  374 us
    unnamed x7, local copies, waits for them, and re-layouts  69.8 us
    pallas_call x1, Pallas kernels, run_tail(): pl.pallas_call(tail_kernel, out_shape=(jax.ShapeDtypeStruct((rows, vocab)...  68.3 us
    another operation x1, local copies, waits for them, and re-layouts, device_step(): w_qkv[0].reshape(width, -1)  16.6 us

profile of v2, /device:TPU:1, one launch (start us, length us, event | category | flops | bytes accessed | tf_op | source)
XLA Modules:
  0.0 532.5 jit_solution(4100519419763155864)
XLA Ops:
  0.6 0.8 copy.19
  1.4 0.1 reshape.41.lens_ref
  1.5 0.0 copy-start
  1.5 1.4 fusion
  3.0 1.1 pad_maximum_fusion
  4.1 15.9 %copy.21 = bf16[1,2048,2752]{2,1,0:T(8,128)(2,1)} copy(bf16[1,2048,2752]{1,2,0:T(8,128)(2,1)} %param.15) | data formatting | bytes 22544384 | tf_op args[3]
  20.1 0.0 copy-done
  20.1 15.4 %copy.22 = bf16[1,2048,2752]{2,1,0:T(8,128)(2,1)} copy(bf16[1,2048,2752]{1,2,0:T(8,128)(2,1)} %param.16) | data formatting | bytes 22544384 | tf_op args[4]
  35.4 16.4 %copy.20 = bf16[1,2048,8,3,128]{1,4,3,2,0:T(8,128)(2,1)} copy(bf16[1,2048,8,3,128]{4,2,3,1,0:T(8,128)(2,1)} %param.13) | data formatting | bytes 25165824 | tf_op args[1]
  51.9 16.6 %copy.23.wqkv_hbm = bf16[2048,3072]{1,0:T(8,128)(2,1)} copy(bf16[2048,3072]{0,1:T(8,128)(2,1)} %bitcast.17) | data formatting | bytes 25165824 | tf_op jit(solution)/shard_map/reshape;squeeze | solution.py:355
  68.5 374.5 %shard_map.139 = (bf16[768,2048]{1,0:T(8,128)(2,1)}, f32[768,8,128]{2,1,0:T(8,128)}, f32[768,8,128]{2,1,0:T(8,128)}) custom-call(s32[768]{0:T(1024)} %copy-done, f32[2,2048]{1,0:T(2,128)} %bitcast.23, f32[768,128]{1,0:T(8,128)} %get-tuple-element.18.cos_ref, f32[768,128]{1,0:T(8,128)} %get-tuple-element.19.sin_ref, bf16[768,2048]{1,0:T(8,128)(2,1)} %bitcast.22, ...), custom_call_target="tpu_custom_call" | custom-call | tf_op jit(solution)/shard_map/pallas_call | solution.py:282
  442.9 21.3 %copy.24.wun_ref = bf16[2048,4000]{1,0:T(8,128)(2,1)} copy(bf16[2048,4000]{0,1:T(8,128)(2,1)} %param.23) | data formatting | bytes 32768000 | tf_op args[11]
  464.2 68.3 %shard_map.140 = (f32[768,4000]{1,0:T(8,128)}, bf16[768,16,8,128]{3,2,1,0:T(8,128)(2,1)}, bf16[768,16,8,128]{3,2,1,0:T(8,128)(2,1)}) custom-call(s32[768]{0:T(1024)} %copy-done, f32[1,2048]{1,0:T(1,128)} %bitcast.24, bf16[768,2048]{1,0:T(8,128)(2,1)} %get-tuple-element.9.final_ref, f32[768,8,128]{2,1,0:T(8,128)} %get-tuple-element.10.knew_ref, ...), custom_call_target="tpu_custom_call" | custom-call | tf_op jit(solution)/shard_map/pallas_call | solution.py:325
  (2 shorter events, 0.0 us)
Async XLA Ops:
  1.5 18.6 %copy-start = (s32[768]{0:T(1024)}, s32[768]{0:T(1024)S(1)}, u32[]{:S(2)}) copy-start(s32[768]{0:T(1024)S(1)} %reshape.41.lens_ref) | copy-start | bytes 9220

commit v3 on v2

--- a/solution.py
+++ b/solution.py
@@ -12,8 +12,11 @@
 MESH = pl.DeviceIdType.MESH
 F32 = jnp.float32
 BF16 = jnp.bfloat16
-MERGE = 3
-TAIL_ROWS = 48
+MERGE = 4
+TAIL_STEPS = 16
+LOG2_E = 1.4426950408889634
+MIN_LENGTH = 4
+ROW_UNROLL = 4
 VMEM_LIMIT = 67043328
 
 
@@ -114,42 +117,41 @@
         unit[...] = rms_norm(xbuf[slot].astype(F32), gain_ref[0:1, :])
         cos_part = cos_ref[span(step), :]
         sin_part = sin_ref[span(step), :]
-        for low, width in column_chunks(wqkv.shape[1], 6 * head_dim):
+        for low, width in column_chunks(wqkv.shape[1], 8 * head_dim):
             proj = dot(unit[...], wqkv[:, low:low + width])
-            for part in range(width // (3 * head_dim)):
-                head = low // (3 * head_dim) + part
-                base = part * 3 * head_dim
-                query = proj[:, base:base + head_dim]
-                key = proj[:, base + head_dim:base + 2 * head_dim]
-                q_scr[:, head, :] = (query * cos_part + pltpu.roll(query, head_dim // 2, 1) * sin_part).astype(BF16).astype(F32)
-                k_scr[:, head, :] = (key * cos_part + pltpu.roll(key, head_dim // 2, 1) * sin_part).astype(BF16).astype(F32)
-                v_scr[:, head, :] = proj[:, base + 2 * head_dim:base + 3 * head_dim].astype(BF16).astype(F32)
+            for part in range(width // head_dim):
+                kind, head = divmod(low // head_dim + part, heads)
+                piece = proj[:, part * head_dim:(part + 1) * head_dim]
+                if kind < 2:
+                    piece = piece * cos_part + pltpu.roll(piece, head_dim // 2, 1) * sin_part
+                (q_scr, k_scr, v_scr)[kind][:, head, :] = piece.astype(BF16).astype(F32)
         for copy in cache_copies(step):
             copy.wait()
         for copy in new_copies(step):
             copy.start()
-        position = lax.broadcasted_iota(jnp.int32, (slots, heads, 1), 0)
+        used = slots - 1
+        position = lax.broadcasted_iota(jnp.int32, (used - MIN_LENGTH, heads, 1), 0) + MIN_LENGTH
 
         def one_row(row):
             length = lens_ref[step * batch + row]
-            query = q_scr[row]
-            scores = jnp.sum(query[None] * kbuf[row].astype(F32), axis=-1, keepdims=True) * scale
-            scores = jnp.where(position < length, scores, -jnp.inf)
-            fresh = jnp.sum(query * k_scr[row], axis=-1, keepdims=True) * scale
+            query = q_scr[row] * (scale * LOG2_E)
+            scores = jnp.sum(query[None] * kbuf[row, :used].astype(F32), axis=-1, keepdims=True)
+            scores = jnp.concatenate([scores[:MIN_LENGTH], jnp.where(position < length, scores[MIN_LENGTH:], -jnp.inf)], axis=0)
+            fresh = jnp.sum(query * k_scr[row], axis=-1, keepdims=True)
             peak = jnp.maximum(jnp.max(scores, axis=0), fresh)
-            exps = jnp.exp(scores - peak[None])
-            fresh_exp = jnp.exp(fresh - peak)
+            exps = jnp.exp2(scores - peak[None])
+            fresh_exp = jnp.exp2(fresh - peak)
             inverse = 1.0 / (jnp.sum(exps, axis=0) + fresh_exp)
             probs = (exps * inverse[None]).astype(BF16).astype(F32)
             fresh_prob = (fresh_exp * inverse).astype(BF16).astype(F32)
-            o_scr[row] = jnp.sum(probs * vbuf[row].astype(F32), axis=0) + fresh_prob * v_scr[row]
+            o_scr[row] = jnp.sum(probs * vbuf[row, :used].astype(F32), axis=0) + fresh_prob * v_scr[row]
 
         def rows_body(index, carry):
-            for sub in range(2):
-                one_row(index * 2 + sub)
+            for sub in range(ROW_UNROLL):
+                one_row(index * ROW_UNROLL + sub)
             return carry
 
-        lax.fori_loop(0, batch // 2, rows_body, 0)
+        lax.fori_loop(0, batch // ROW_UNROLL, rows_body, 0)
 
         @pl.when(step + 1 < count)
         def _():
@@ -298,9 +300,14 @@
     )(lens, gains, cos_part, sin_part, embeds, wqkv, wout, wgate, wup, wdown, k_cache, v_cache)
 
 
-def tail_kernel(lens_ref, gain_ref, final_ref, knew_ref, vnew_ref, kc_ref, vc_ref, wun_ref, logits_ref, ko_ref, vo_ref):
+def tail_kernel(lens_ref, gain_ref, final_ref, knew_ref, vnew_ref, kc_ref, vc_ref, wun_ref, logits_ref, ko_ref, vo_ref, normed):
     block = pl.program_id(0)
     rows = kc_ref.shape[0]
+
+    @pl.when(block == 0)
+    def _():
+        normed[...] = rms_norm(final_ref[...].astype(F32), gain_ref[...])
+
     ko_ref[...] = kc_ref[...]
     vo_ref[...] = vc_ref[...]
 
@@ -311,26 +318,27 @@
         return carry
 
     lax.fori_loop(0, rows, place, 0)
-    normed = rms_norm(final_ref[...].astype(F32), gain_ref[...])
-    for low, width in column_chunks(wun_ref.shape[1], 1024):
-        logits_ref[:, low:low + width] = dot(normed, wun_ref[:, low:low + width])
+    logits_ref[...] = lax.dot_general(normed[...], wun_ref[...], (((1,), (1,)), ((), ())), preferred_element_type=F32)
 
 
 def run_tail(lens, gain, final, knew, vnew, k_cache, v_cache, wun):
     rows, width = final.shape
     slots, heads, head_dim = k_cache.shape[1:]
-    vocab = wun.shape[1]
-    cache_spec = pl.BlockSpec((TAIL_ROWS, slots, heads, head_dim), lambda i, lens: (i, 0, 0, 0))
-    new_spec = pl.BlockSpec((TAIL_ROWS, heads, head_dim), lambda i, lens: (i, 0, 0))
+    vocab = wun.shape[0]
+    block = rows // TAIL_STEPS
+    columns = pl.cdiv(vocab, TAIL_STEPS * 128) * 128
+    cache_spec = pl.BlockSpec((block, slots, heads, head_dim), lambda i, lens: (i, 0, 0, 0))
+    new_spec = pl.BlockSpec((block, heads, head_dim), lambda i, lens: (i, 0, 0))
     return pl.pallas_call(
         tail_kernel,
         out_shape=(jax.ShapeDtypeStruct((rows, vocab), F32), jax.ShapeDtypeStruct(k_cache.shape, BF16), jax.ShapeDtypeStruct(v_cache.shape, BF16)),
         grid_spec=pltpu.PrefetchScalarGridSpec(
             num_scalar_prefetch=1,
-            grid=(rows // TAIL_ROWS,),
-            in_specs=[pl.BlockSpec((1, width), lambda i, lens: (0, 0)), pl.BlockSpec((TAIL_ROWS, width), lambda i, lens: (i, 0)), new_spec, new_spec, cache_spec, cache_spec,
-                      pl.BlockSpec((width, vocab), lambda i, lens: (0, 0), pipeline_mode=pl.Buffered(1))],
-            out_specs=(pl.BlockSpec((TAIL_ROWS, vocab), lambda i, lens: (i, 0)), cache_spec, cache_spec),
+            grid=(TAIL_STEPS,),
+            in_specs=[pl.BlockSpec((1, width), lambda i, lens: (0, 0)), pl.BlockSpec((rows, width), lambda i, lens: (0, 0)), new_spec, new_spec, cache_spec, cache_spec,
+                      pl.BlockSpec((columns, width), lambda i, lens: (i, 0))],
+            out_specs=(pl.BlockSpec((rows, columns), lambda i, lens: (0, i)), cache_spec, cache_spec),
+            scratch_shapes=[pltpu.VMEM((rows, width), BF16)],
         ),
         compiler_params=pltpu.CompilerParams(dimension_semantics=("arbitrary",), vmem_limit_bytes=VMEM_LIMIT),
     )(lens, gain, final, knew, vnew, k_cache, v_cache, wun)
@@ -352,8 +360,8 @@
         k_rows = k_cache.reshape((rows,) + cache_shape[3:])
         v_rows = v_cache.reshape((rows,) + cache_shape[3:])
         final, knew, vnew = run_pipeline(
-            stages, lens, norm_gain[0], cos_part, sin_part, embeds.reshape(rows, width), w_qkv[0].reshape(width, -1), w_out[0], w_gate[0], w_up[0], w_down[0], k_rows, v_rows)
-        logits, k_out, v_out = run_tail(lens, final_gain.reshape(1, width), final, knew, vnew, k_rows, v_rows, w_unembed)
+            stages, lens, norm_gain[0], cos_part, sin_part, embeds.reshape(rows, width), w_qkv[0].transpose(0, 2, 1, 3).reshape(width, -1), w_out[0], w_gate[0], w_up[0], w_down[0], k_rows, v_rows)
+        logits, k_out, v_out = run_tail(lens, final_gain.reshape(1, width), final, knew, vnew, k_rows, v_rows, w_unembed.T)
         return logits.reshape(groups, seqs, -1), k_out.reshape(cache_shape), v_out.reshape(cache_shape)
 
     return jax.shard_map(device_step, mesh=mesh, in_specs=in_specs, out_specs=out_specs, check_vma=False)

time: 535 us -> 438 us (0.82)
  Pallas kernels: 443 us -> 389 us
  local copies, waits for them, and re-layouts: 86.5 us -> 44.6 us
    pallas_call x1, Pallas kernels: 374 us -> 336 us  [run_pipeline(): pl.pallas_call(functools.partial(pipeline_kernel, stages, batch), out_sha...]
    unnamed x7 -> x6, local copies, waits for them, and re-layouts: 69.8 us -> 44.5 us
    another operation x1 -> x0, local copies, waits for them, and re-layouts: 16.6 us -> none  [device_step(): w_qkv[0].reshape(width, -1)]
    pallas_call x1, Pallas kernels: 68.3 us -> 53.2 us  [run_tail(): pl.pallas_call(tail_kernel, out_shape=(jax.ShapeDtypeStruct((rows, vocab)...]
where the time goes in v3:
time: 438 us; the launch traced here: 437 us
  Pallas kernels  389 us (89%)
  local copies, waits for them, and re-layouts  44.6 us (10%)
    pallas_call x1, Pallas kernels, run_pipeline(): pl.pallas_call(functools.partial(pipeline_kernel, stages, batch), out_sha...  336 us
    pallas_call x1, Pallas kernels, run_tail(): pl.pallas_call(tail_kernel, out_shape=(jax.ShapeDtypeStruct((rows, vocab)...  53.2 us
    unnamed x6, local copies, waits for them, and re-layouts  44.5 us

profile of v3, /device:TPU:1, one launch (start us, length us, event | category | flops | bytes accessed | tf_op | source)
XLA Modules:
  0.0 437.0 jit_solution(8651836666803914405)
XLA Ops:
  0.6 0.8 copy.17
  1.4 0.1 reshape.44.lens_ref
  1.5 0.0 copy-start
  1.5 1.4 fusion
  3.0 1.2 pad_maximum_fusion
  4.1 15.9 %copy.18 = bf16[1,2048,2752]{2,1,0:T(8,128)(2,1)} copy(bf16[1,2048,2752]{1,2,0:T(8,128)(2,1)} %param.15) | data formatting | bytes 22544384 | tf_op args[3]
  20.1 0.0 copy-done
  20.1 15.9 %copy.19 = bf16[1,2048,2752]{2,1,0:T(8,128)(2,1)} copy(bf16[1,2048,2752]{1,2,0:T(8,128)(2,1)} %param.16) | data formatting | bytes 22544384 | tf_op args[4]
  36.0 11.8 %copy.22 = bf16[256,8,24,128]{3,1,2,0:T(8,128)(2,1)} copy(bf16[256,8,24,128]{3,2,1,0:T(8,128)(2,1)} %bitcast.29) | data formatting | bytes 25165824
  47.8 335.9 %shard_map.139 = (bf16[768,2048]{1,0:T(8,128)(2,1)}, f32[768,8,128]{2,1,0:T(8,128)}, f32[768,8,128]{2,1,0:T(8,128)}) custom-call(s32[768]{0:T(1024)} %copy-done, f32[2,2048]{1,0:T(2,128)} %bitcast.33, f32[768,128]{1,0:T(8,128)} %get-tuple-element.18.cos_ref, f32[768,128]{1,0:T(8,128)} %get-tuple-element.19.sin_ref, bf16[768,2048]{1,0:T(8,128)(2,1)} %bitcast.32, ...), custom_call_target="tpu_custom_call" | custom-call | tf_op jit(solution)/shard_map/pallas_call | solution.py:284
  383.8 53.2 %shard_map.140 = (f32[768,4000]{1,0:T(8,128)}, bf16[768,16,8,128]{3,2,1,0:T(8,128)(2,1)}, bf16[768,16,8,128]{3,2,1,0:T(8,128)(2,1)}) custom-call(s32[768]{0:T(1024)} %copy-done, f32[1,2048]{1,0:T(1,128)} %bitcast.34, bf16[768,2048]{1,0:T(8,128)(2,1)} %get-tuple-element.9.final_ref, f32[768,8,128]{2,1,0:T(8,128)} %get-tuple-element.10.knew_ref, ...), custom_call_target="tpu_custom_call" | custom-call | tf_op jit(solution)/shard_map/pallas_call | solution.py:332
  (2 shorter events, 0.0 us)
Async XLA Ops:
  1.5 18.6 %copy-start = (s32[768]{0:T(1024)}, s32[768]{0:T(1024)S(1)}, u32[]{:S(2)}) copy-start(s32[768]{0:T(1024)S(1)} %reshape.44.lens_ref) | copy-start | bytes 9220

commit v4 on v3

--- a/solution.py
+++ b/solution.py
@@ -15,8 +15,7 @@
 MERGE = 4
 TAIL_STEPS = 16
 LOG2_E = 1.4426950408889634
-MIN_LENGTH = 4
-ROW_UNROLL = 4
+ROW_UNROLL = 16
 VMEM_LIMIT = 67043328
 
 
@@ -130,28 +129,34 @@
         for copy in new_copies(step):
             copy.start()
         used = slots - 1
-        position = lax.broadcasted_iota(jnp.int32, (used - MIN_LENGTH, heads, 1), 0) + MIN_LENGTH
-
-        def one_row(row):
-            length = lens_ref[step * batch + row]
-            query = q_scr[row] * (scale * LOG2_E)
-            scores = jnp.sum(query[None] * kbuf[row, :used].astype(F32), axis=-1, keepdims=True)
-            scores = jnp.concatenate([scores[:MIN_LENGTH], jnp.where(position < length, scores[MIN_LENGTH:], -jnp.inf)], axis=0)
-            fresh = jnp.sum(query * k_scr[row], axis=-1, keepdims=True)
-            peak = jnp.maximum(jnp.max(scores, axis=0), fresh)
-            exps = jnp.exp2(scores - peak[None])
-            fresh_exp = jnp.exp2(fresh - peak)
-            inverse = 1.0 / (jnp.sum(exps, axis=0) + fresh_exp)
-            probs = (exps * inverse[None]).astype(BF16).astype(F32)
-            fresh_prob = (fresh_exp * inverse).astype(BF16).astype(F32)
-            o_scr[row] = jnp.sum(probs * vbuf[row, :used].astype(F32), axis=0) + fresh_prob * v_scr[row]
-
-        def rows_body(index, carry):
+        lane = lax.broadcasted_iota(jnp.int32, (heads, head_dim), 1)
+
+        def score_rows(index, carry):
+            group = pl.ds(index * ROW_UNROLL, ROW_UNROLL)
+            query = q_scr[group] * (scale * LOG2_E)
+            packed = jnp.where(lane == used, jnp.sum(query * k_scr[group], axis=-1, keepdims=True), -jnp.inf)
+            for slot_idx in range(used):
+                packed = jnp.where(lane == slot_idx, jnp.sum(query * kbuf[group, slot_idx].astype(F32), axis=-1, keepdims=True), packed)
             for sub in range(ROW_UNROLL):
-                one_row(index * ROW_UNROLL + sub)
+                length = lens_ref[step * batch + index * ROW_UNROLL + sub]
+                q_scr[index * ROW_UNROLL + sub] = jnp.where(jnp.logical_or(lane < length, lane == used), packed[sub], -jnp.inf)
             return carry
 
-        lax.fori_loop(0, batch // ROW_UNROLL, rows_body, 0)
+        lax.fori_loop(0, batch // ROW_UNROLL, score_rows, 0)
+        packed = q_scr[...]
+        exps = jnp.exp2(packed - jnp.max(packed, axis=-1, keepdims=True))
+        q_scr[...] = (exps * (1.0 / jnp.sum(exps, axis=-1, keepdims=True))).astype(BF16).astype(F32)
+
+        def value_rows(index, carry):
+            group = pl.ds(index * ROW_UNROLL, ROW_UNROLL)
+            probs = q_scr[group]
+            total = probs[:, :, used:used + 1] * v_scr[group]
+            for slot_idx in range(used):
+                total = total + probs[:, :, slot_idx:slot_idx + 1] * vbuf[group, slot_idx].astype(F32)
+            o_scr[group] = total
+            return carry
+
+        lax.fori_loop(0, batch // ROW_UNROLL, value_rows, 0)
 
         @pl.when(step + 1 < count)
         def _():

time: 438 us -> 425 us (0.970)
  Pallas kernels: 389 us -> 376 us
    pallas_call x1, Pallas kernels: 336 us -> 323 us  [run_pipeline(): pl.pallas_call(functools.partial(pipeline_kernel, stages, batch), out_sha...]
where the time goes in v4:
time: 425 us; the launch traced here: 424 us
  Pallas kernels  376 us (88%)
  local copies, waits for them, and re-layouts  44.6 us (10%)
    pallas_call x1, Pallas kernels, run_pipeline(): pl.pallas_call(functools.partial(pipeline_kernel, stages, batch), out_sha...  323 us
    pallas_call x1, Pallas kernels, run_tail(): pl.pallas_call(tail_kernel, out_shape=(jax.ShapeDtypeStruct((rows, vocab)...  53.2 us
    unnamed x6, local copies, waits for them, and re-layouts  44.5 us

profile of v4, /device:TPU:1, one launch (start us, length us, event | category | flops | bytes accessed | tf_op | source)
XLA Modules:
  0.0 424.0 jit_solution(18425443897757705943)
XLA Ops:
  0.6 0.8 copy.17
  1.4 0.1 reshape.44.lens_ref
  1.5 0.0 copy-start
  1.5 1.4 fusion
  3.0 1.2 pad_maximum_fusion
  4.1 15.9 %copy.18 = bf16[1,2048,2752]{2,1,0:T(8,128)(2,1)} copy(bf16[1,2048,2752]{1,2,0:T(8,128)(2,1)} %param.15) | data formatting | bytes 22544384 | tf_op args[3]
  20.1 0.0 copy-done
  20.1 15.9 %copy.19 = bf16[1,2048,2752]{2,1,0:T(8,128)(2,1)} copy(bf16[1,2048,2752]{1,2,0:T(8,128)(2,1)} %param.16) | data formatting | bytes 22544384 | tf_op args[4]
  36.0 11.8 %copy.22 = bf16[256,8,24,128]{3,1,2,0:T(8,128)(2,1)} copy(bf16[256,8,24,128]{3,2,1,0:T(8,128)(2,1)} %bitcast.29) | data formatting | bytes 25165824
  47.8 323.0 %shard_map.139 = (bf16[768,2048]{1,0:T(8,128)(2,1)}, f32[768,8,128]{2,1,0:T(8,128)}, f32[768,8,128]{2,1,0:T(8,128)}) custom-call(s32[768]{0:T(1024)} %copy-done, f32[2,2048]{1,0:T(2,128)} %bitcast.33, f32[768,128]{1,0:T(8,128)} %get-tuple-element.18.cos_ref, f32[768,128]{1,0:T(8,128)} %get-tuple-element.19.sin_ref, bf16[768,2048]{1,0:T(8,128)(2,1)} %bitcast.32, ...), custom_call_target="tpu_custom_call" | custom-call | tf_op jit(solution)/shard_map/pallas_call | solution.py:289
  370.8 53.2 %shard_map.140 = (f32[768,4000]{1,0:T(8,128)}, bf16[768,16,8,128]{3,2,1,0:T(8,128)(2,1)}, bf16[768,16,8,128]{3,2,1,0:T(8,128)(2,1)}) custom-call(s32[768]{0:T(1024)} %copy-done, f32[1,2048]{1,0:T(1,128)} %bitcast.34, bf16[768,2048]{1,0:T(8,128)(2,1)} %get-tuple-element.9.final_ref, f32[768,8,128]{2,1,0:T(8,128)} %get-tuple-element.10.knew_ref, ...), custom_call_target="tpu_custom_call" | custom-call | tf_op jit(solution)/shard_map/pallas_call | solution.py:337
  (2 shorter events, 0.0 us)
Async XLA Ops:
  1.5 18.6 %copy-start = (s32[768]{0:T(1024)}, s32[768]{0:T(1024)S(1)}, u32[]{:S(2)}) copy-start(s32[768]{0:T(1024)S(1)} %reshape.44.lens_ref) | copy-start | bytes 9220

commit v5 on v4

--- a/solution.py
+++ b/solution.py
@@ -16,6 +16,7 @@
 TAIL_STEPS = 16
 LOG2_E = 1.4426950408889634
 ROW_UNROLL = 16
+CHUNKS = 2
 VMEM_LIMIT = 67043328
 
 
@@ -33,6 +34,10 @@
 
 def column_chunks(total, width):
     return [(low, min(width, total - low)) for low in range(0, total, width)]
+
+
+def joined(ref, slot):
+    return jnp.concatenate([ref[slot, chunk].astype(F32) for chunk in range(CHUNKS)], axis=-1)
 
 
 def dot(lhs, rhs):
@@ -68,9 +73,9 @@
     def new_copies(step):
         return (pltpu.make_async_copy(k_scr, knew_ref.at[span(step)], n_sem.at[0]), pltpu.make_async_copy(v_scr, vnew_ref.at[span(step)], n_sem.at[1]))
 
-    def sum_copy(step, send, recv, send_sem, recv_sem):
-        slot = lax.rem(step, 2)
-        return pltpu.make_async_remote_copy(send.at[slot], recv.at[slot], send_sem.at[slot], recv_sem.at[slot], device_id=peer, device_id_type=MESH)
+    def sum_copy(step, chunk, send, recv, send_sem, recv_sem):
+        out, into = lax.rem(step, 2), lax.rem(step, 3)
+        return pltpu.make_async_remote_copy(send.at[out, chunk], recv.at[into, chunk], send_sem.at[out, chunk], recv_sem.at[into, chunk], device_id=peer, device_id_type=MESH)
 
     def hop_copy(step):
         slot = lax.rem(step, 2)
@@ -172,11 +177,11 @@
 
         for head in range(heads):
             attn[:, head * head_dim:(head + 1) * head_dim] = o_scr[:, head, :].astype(BF16)
-        for low, width in column_chunks(wout.shape[1], 1024):
+        for chunk, (low, width) in enumerate(column_chunks(wout.shape[1], wout.shape[1] // CHUNKS)):
             partial = dot(attn[...], wout[:, low:low + width])
-            send_a[slot, :, low:low + width] = partial.astype(BF16)
-            resid[slot, :, low:low + width] = xbuf[slot, :, low:low + width].astype(F32) + partial
-        sum_copy(step, send_a, recv_a, a_send, a_recv).start()
+            send_a[slot, chunk] = partial.astype(BF16)
+            resid[lax.rem(step, 3), :, low:low + width] = xbuf[slot, :, low:low + width].astype(F32) + partial
+            sum_copy(step, chunk, send_a, recv_a, a_send, a_recv).start()
 
         @pl.when(jnp.logical_and(stage == 0, step + 2 < count))
         def _():
@@ -194,23 +199,26 @@
             for copy in weights[2:]:
                 copy.wait()
 
-        sum_copy(step, send_a, recv_a, a_send, a_recv).wait()
-        summed = resid[slot] + recv_a[slot].astype(F32)
-        resid[slot] = summed
+        kept = lax.rem(step, 3)
+        for chunk in range(CHUNKS):
+            sum_copy(step, chunk, send_a, recv_a, a_send, a_recv).wait()
+        summed = resid[kept] + joined(recv_a, kept)
+        resid[kept] = summed
         unit[...] = rms_norm(summed, gain_ref[1:2, :])
         for low, width in column_chunks(wgate.shape[1], 768):
             gate = dot(unit[...], wgate[:, low:low + width])
             up = dot(unit[...], wup[:, low:low + width])
             hidden[:, low:low + width] = (jax.nn.silu(gate) * up).astype(BF16)
-        for low, width in column_chunks(wdown.shape[1], 1024):
+        for chunk, (low, width) in enumerate(column_chunks(wdown.shape[1], wdown.shape[1] // CHUNKS)):
             partial = dot(hidden[...], wdown[:, low:low + width])
-            send_d[slot, :, low:low + width] = partial.astype(BF16)
-            resid[slot, :, low:low + width] = resid[slot, :, low:low + width] + partial
-        sum_copy(step, send_d, recv_d, d_send, d_recv).start()
+            send_d[slot, chunk] = partial.astype(BF16)
+            resid[kept, :, low:low + width] = resid[kept, :, low:low + width] + partial
+            sum_copy(step, chunk, send_d, recv_d, d_send, d_recv).start()
 
     def hand_on(step):
         slot = lax.rem(step, 2)
-        sum_copy(step, send_d, recv_d, d_send, d_recv).wait()
+        for chunk in range(CHUNKS):
+            sum_copy(step, chunk, send_d, recv_d, d_send, d_recv).wait()
 
         @pl.when(jnp.logical_and(stage < last, step >= 2))
         def _():
@@ -223,7 +231,8 @@
                 copy.wait_send()
             final_local(step - 2).wait()
 
-        xout[slot] = (resid[slot] + recv_d[slot].astype(F32)).astype(BF16)
+        kept = lax.rem(step, 3)
+        xout[slot] = (resid[kept] + joined(recv_d, kept)).astype(BF16)
 
         @pl.when(stage < last)
         def _():
@@ -240,13 +249,13 @@
         def _():
             attend(step)
 
+        @pl.when(step < count)
+        def _():
+            project(step)
+
         @pl.when(step >= 2)
         def _():
             hand_on(step - 2)
-
-        @pl.when(step < count)
-        def _():
-            project(step)
 
         @pl.when(jnp.logical_and(step >= 1, step <= count))
         def _():
@@ -284,7 +293,8 @@
     count = rows // batch
     anywhere = pl.BlockSpec(memory_space=pl.ANY)
     local = pl.BlockSpec(memory_space=pltpu.VMEM)
-    pair = pltpu.SemaphoreType.DMA((2,))
+    pair, sent, landed = pltpu.SemaphoreType.DMA((2,)), pltpu.SemaphoreType.DMA((2, CHUNKS)), pltpu.SemaphoreType.DMA((3, CHUNKS))
+    part = (CHUNKS, batch, width // CHUNKS)
     new_rows = jax.ShapeDtypeStruct((rows, heads, head_dim), F32)
     return pl.pallas_call(
         functools.partial(pipeline_kernel, stages, batch),
@@ -294,36 +304,66 @@
         scratch_shapes=[
             pltpu.VMEM(wqkv.shape, BF16), pltpu.VMEM(wout.shape, BF16), pltpu.VMEM(wgate.shape, BF16), pltpu.VMEM(wup.shape, BF16), pltpu.VMEM(wdown.shape, BF16),
             pltpu.VMEM((batch, slots, heads, head_dim), BF16), pltpu.VMEM((batch, slots, heads, head_dim), BF16),
-            pltpu.VMEM((2, batch, width), BF16), pltpu.VMEM((2, batch, width), BF16), pltpu.VMEM((2, batch, width), F32),
-            pltpu.VMEM((2, batch, width), BF16), pltpu.VMEM((2, batch, width), BF16), pltpu.VMEM((2, batch, width), BF16), pltpu.VMEM((2, batch, width), BF16),
+            pltpu.VMEM((2, batch, width), BF16), pltpu.VMEM((2, batch, width), BF16), pltpu.VMEM((3, batch, width), F32),
+            pltpu.VMEM((2,) + part, BF16), pltpu.VMEM((3,) + part, BF16), pltpu.VMEM((2,) + part, BF16), pltpu.VMEM((3,) + part, BF16),
             pltpu.VMEM((batch, width), BF16), pltpu.VMEM((batch, wgate.shape[1]), BF16), pltpu.VMEM((batch, heads * head_dim), BF16),
             pltpu.VMEM((batch, heads, head_dim), F32), pltpu.VMEM((batch, heads, head_dim), F32), pltpu.VMEM((batch, heads, head_dim), F32), pltpu.VMEM((batch, heads, head_dim), F32),
-            pltpu.SemaphoreType.DMA((5,)), pair, pair, pair, pair, pair, pair, pair, pair, pair,
+            pltpu.SemaphoreType.DMA((5,)), pair, pair, pair, sent, landed, sent, landed, pair, pair,
             pltpu.SemaphoreType.DMA((2, stages)), pltpu.SemaphoreType.DMA((count,)), pltpu.SemaphoreType.REGULAR,
         ],
         compiler_params=pltpu.CompilerParams(has_side_effects=True, vmem_limit_bytes=VMEM_LIMIT),
     )(lens, gains, cos_part, sin_part, embeds, wqkv, wout, wgate, wup, wdown, k_cache, v_cache)
 
 
-def tail_kernel(lens_ref, gain_ref, final_ref, knew_ref, vnew_ref, kc_ref, vc_ref, wun_ref, logits_ref, ko_ref, vo_ref, normed):
+def tail_kernel(lens_ref, gain_ref, final_ref, knew_ref, vnew_ref, kc_hbm, vc_hbm, wun_ref, logits_ref, ko_hbm, vo_hbm, normed, kring, vring, in_sem, out_sem):
     block = pl.program_id(0)
-    rows = kc_ref.shape[0]
+    steps = pl.num_programs(0)
+    rows = kring.shape[1]
+
+    def reads(step):
+        slot, span = lax.rem(step, 3), pl.ds(step * rows, rows)
+        return [pltpu.make_async_copy(src.at[span], ring.at[slot], in_sem.at[i, slot]) for i, (src, ring) in enumerate([(kc_hbm, kring), (vc_hbm, vring)])]
+
+    def writes(step):
+        slot, span = lax.rem(step, 3), pl.ds(step * rows, rows)
+        return [pltpu.make_async_copy(ring.at[slot], dst.at[span], out_sem.at[i, slot]) for i, (dst, ring) in enumerate([(ko_hbm, kring), (vo_hbm, vring)])]
 
     @pl.when(block == 0)
     def _():
+        for copy in reads(0) + reads(1):
+            copy.start()
         normed[...] = rms_norm(final_ref[...].astype(F32), gain_ref[...])
 
-    ko_ref[...] = kc_ref[...]
-    vo_ref[...] = vc_ref[...]
+    for copy in reads(block):
+        copy.wait()
+    slot = lax.rem(block, 3)
 
     def place(row, carry):
         length = lens_ref[block * rows + row]
-        ko_ref[row, length] = knew_ref[row].astype(BF16)
-        vo_ref[row, length] = vnew_ref[row].astype(BF16)
+        kring[slot, row, length] = knew_ref[row].astype(BF16)
+        vring[slot, row, length] = vnew_ref[row].astype(BF16)
         return carry
 
-    lax.fori_loop(0, rows, place, 0)
+    lax.fori_loop(0, rows, place, 0, unroll=4)
+    for copy in writes(block):
+        copy.start()
+
+    @pl.when(block > 0)
+    def _():
+        for copy in writes(block - 1):
+            copy.wait()
+
+    @pl.when(block + 2 < steps)
+    def _():
+        for copy in reads(block + 2):
+            copy.start()
+
     logits_ref[...] = lax.dot_general(normed[...], wun_ref[...], (((1,), (1,)), ((), ())), preferred_element_type=F32)
+
+    @pl.when(block == steps - 1)
+    def _():
+        for copy in writes(block):
+            copy.wait()
 
 
 def run_tail(lens, gain, final, knew, vnew, k_cache, v_cache, wun):
@@ -332,7 +372,8 @@
     vocab = wun.shape[0]
     block = rows // TAIL_STEPS
     columns = pl.cdiv(vocab, TAIL_STEPS * 128) * 128
-    cache_spec = pl.BlockSpec((block, slots, heads, head_dim), lambda i, lens: (i, 0, 0, 0))
+    cache_spec = pl.BlockSpec(memory_space=pl.ANY)
+    ring = pltpu.VMEM((3, block, slots, heads, head_dim), BF16)
     new_spec = pl.BlockSpec((block, heads, head_dim), lambda i, lens: (i, 0, 0))
     return pl.pallas_call(
         tail_kernel,
@@ -343,7 +384,7 @@
             in_specs=[pl.BlockSpec((1, width), lambda i, lens: (0, 0)), pl.BlockSpec((rows, width), lambda i, lens: (0, 0)), new_spec, new_spec, cache_spec, cache_spec,
                       pl.BlockSpec((columns, width), lambda i, lens: (i, 0))],
             out_specs=(pl.BlockSpec((rows, columns), lambda i, lens: (0, i)), cache_spec, cache_spec),
-            scratch_shapes=[pltpu.VMEM((rows, width), BF16)],
+            scratch_shapes=[pltpu.VMEM((rows, width), BF16), ring, ring, pltpu.SemaphoreType.DMA((2, 3)), pltpu.SemaphoreType.DMA((2, 3))],
         ),
         compiler_params=pltpu.CompilerParams(dimension_semantics=("arbitrary",), vmem_limit_bytes=VMEM_LIMIT),
     )(lens, gain, final, knew, vnew, k_cache, v_cache, wun)

time: 425 us -> 397 us (0.934)
  Pallas kernels: 376 us -> 348 us
    pallas_call x1, Pallas kernels: 323 us -> 301 us  [run_pipeline(): pl.pallas_call(functools.partial(pipeline_kernel, stages, batch), out_sha...]
    pallas_call x1, Pallas kernels: 53.2 us -> 47.1 us  [run_tail(): pl.pallas_call(tail_kernel, out_shape=(jax.ShapeDtypeStruct((rows, vocab)...]
where the time goes in v5:
time: 397 us; the launch traced here: 396 us
  Pallas kernels  348 us (88%)
  local copies, waits for them, and re-layouts  44.6 us (11%)
    pallas_call x1, Pallas kernels, run_pipeline(): pl.pallas_call(functools.partial(pipeline_kernel, stages, batch), out_sha...  301 us
    pallas_call x1, Pallas kernels, run_tail(): pl.pallas_call(tail_kernel, out_shape=(jax.ShapeDtypeStruct((rows, vocab)...  47.1 us
    unnamed x6, local copies, waits for them, and re-layouts  44.5 us

profile of v5, /device:TPU:1, one launch (start us, length us, event | category | flops | bytes accessed | tf_op | source)
XLA Modules:
  0.0 396.1 jit_solution(15985728038444913676)
XLA Ops:
  0.6 0.8 copy.17
  1.4 0.1 reshape.44.lens_ref
  1.5 0.0 copy-start
  1.5 1.4 fusion
  3.0 1.2 pad_maximum_fusion
  4.1 15.9 %copy.18 = bf16[1,2048,2752]{2,1,0:T(8,128)(2,1)} copy(bf16[1,2048,2752]{1,2,0:T(8,128)(2,1)} %param.15) | data formatting | bytes 22544384 | tf_op args[3]
  20.1 0.0 copy-done
  20.1 15.9 %copy.19 = bf16[1,2048,2752]{2,1,0:T(8,128)(2,1)} copy(bf16[1,2048,2752]{1,2,0:T(8,128)(2,1)} %param.16) | data formatting | bytes 22544384 | tf_op args[4]
  36.0 11.8 %copy.22 = bf16[256,8,24,128]{3,1,2,0:T(8,128)(2,1)} copy(bf16[256,8,24,128]{3,2,1,0:T(8,128)(2,1)} %bitcast.29) | data formatting | bytes 25165824
  47.8 301.2 %shard_map.139 = (bf16[768,2048]{1,0:T(8,128)(2,1)}, f32[768,8,128]{2,1,0:T(8,128)}, f32[768,8,128]{2,1,0:T(8,128)}) custom-call(s32[768]{0:T(1024)} %copy-done, f32[2,2048]{1,0:T(2,128)} %bitcast.33, f32[768,128]{1,0:T(8,128)} %get-tuple-element.18.cos_ref, f32[768,128]{1,0:T(8,128)} %get-tuple-element.19.sin_ref, bf16[768,2048]{1,0:T(8,128)(2,1)} %bitcast.32, ...), custom_call_target="tpu_custom_call" | custom-call | tf_op jit(solution)/shard_map/pallas_call | solution.py:299
  349.0 47.1 %shard_map.140 = (f32[768,4000]{1,0:T(8,128)}, bf16[768,16,8,128]{3,2,1,0:T(8,128)(2,1)}, bf16[768,16,8,128]{3,2,1,0:T(8,128)(2,1)}) custom-call(s32[768]{0:T(1024)} %copy-done, f32[1,2048]{1,0:T(1,128)} %bitcast.34, bf16[768,2048]{1,0:T(8,128)(2,1)} %get-tuple-element.9.final_ref, f32[768,8,128]{2,1,0:T(8,128)} %get-tuple-element.10.knew_ref, ...), custom_call_target="tpu_custom_call" | custom-call | tf_op jit(solution)/shard_map/pallas_call | solution.py:378
  (2 shorter events, 0.0 us)
Async XLA Ops:
  1.5 18.6 %copy-start = (s32[768]{0:T(1024)}, s32[768]{0:T(1024)S(1)}, u32[]{:S(2)}) copy-start(s32[768]{0:T(1024)S(1)} %reshape.44.lens_ref) | copy-start | bytes 9220

commit v6 on v5

--- a/solution.py
+++ b/solution.py
@@ -17,6 +17,7 @@
 LOG2_E = 1.4426950408889634
 ROW_UNROLL = 16
 CHUNKS = 2
+TILE = 256
 VMEM_LIMIT = 67043328
 
 
@@ -47,8 +48,8 @@
 def pipeline_kernel(
     stages, batch, lens_ref, gain_ref, cos_ref, sin_ref, emb_ref, wqkv_hbm, wout_hbm, wgate_hbm, wup_hbm, wdown_hbm, kc_hbm, vc_hbm,
     final_ref, knew_ref, vnew_ref,
-    wqkv, wout, wgate, wup, wdown, kbuf, vbuf, xbuf, xout, resid, send_a, recv_a, send_d, recv_d, unit, hidden, attn, q_scr, k_scr, v_scr, o_scr,
-    w_sem, c_sem, n_sem, e_sem, a_send, a_recv, d_send, d_recv, x_send, x_recv, f_send, f_recv, credit,
+    wqkv, wout, wgate, wup, wdown, kbuf, vbuf, xbuf, xout, resid, send_a, recv_a, send_d, recv_d, unit, hidden, attn, q_scr, k_scr, v_scr, o_scr, eye,
+    w_sem, t_sem, c_sem, n_sem, e_sem, a_send, a_recv, d_send, d_recv, x_send, x_recv, f_send, f_recv, credit,
 ):
     stage = lax.axis_index("stage")
     peer = {"tp": 1 - lax.axis_index("tp")}
@@ -58,8 +59,31 @@
     heads, head_dim = kbuf.shape[2], kbuf.shape[3]
     slots = kbuf.shape[1]
     scale = head_dim ** -0.5
-    weights = [pltpu.make_async_copy(src, dst, w_sem.at[i]) for i, (src, dst) in enumerate(
-        [(wqkv_hbm, wqkv), (wout_hbm, wout), (wgate_hbm, wgate), (wup_hbm, wup), (wdown_hbm, wdown)])]
+    weights = [pltpu.make_async_copy(src, dst, w_sem.at[i]) for i, (src, dst) in enumerate([(wqkv_hbm, wqkv), (wout_hbm, wout)])]
+    whole, rest = divmod(wdown.shape[0], TILE)
+
+    def block_copy(src, index, size=TILE):
+        lines = pl.ds(index * TILE, size)
+        return pltpu.make_async_copy(src.at[lines], wdown.at[lines], t_sem.at[index])
+
+    def each_block(action):
+        def body(index, carry):
+            action(pl.multiple_of(index * TILE, TILE), index, TILE)
+            return carry
+
+        lax.fori_loop(0, whole, body, 0)
+        if rest:
+            action(whole * TILE, whole, rest)
+
+    def turn(src, dst, following):
+        def action(low, index, size):
+            block_copy(src, index, size).wait()
+            for col in range(0, wdown.shape[1], TILE):
+                turned = lax.dot_general(eye[...], wdown[pl.ds(low, size), col:col + TILE], (((1,), (1,)), ((), ())), preferred_element_type=F32)
+                dst[col:col + TILE, pl.ds(low, size)] = turned.astype(BF16)
+            block_copy(following, index, size).start()
+
+        each_block(action)
 
     def span(step):
         return pl.ds(pl.multiple_of(step * batch, batch), batch)
@@ -90,6 +114,7 @@
         slot = lax.rem(step, 2)
         return pltpu.make_async_copy(xout.at[slot], final_ref.at[span(step)], f_send.at[slot, last])
 
+    each_block(lambda low, index, size: block_copy(wgate_hbm, index, size).start())
     for copy in weights[:1] + list(cache_copies(0)) + weights[1:]:
         copy.start()
 
@@ -196,8 +221,7 @@
 
         @pl.when(step == 0)
         def _():
-            for copy in weights[2:]:
-                copy.wait()
+            each_block(lambda low, index, size: block_copy(wdown_hbm, index, size).wait())
 
         kept = lax.rem(step, 3)
         for chunk in range(CHUNKS):
@@ -263,6 +287,9 @@
 
         return carry
 
+    eye[...] = (lax.broadcasted_iota(jnp.int32, eye.shape, 0) == lax.broadcasted_iota(jnp.int32, eye.shape, 1)).astype(F32).astype(BF16)
+    turn(wgate_hbm, wgate, wup_hbm)
+    turn(wup_hbm, wup, wdown_hbm)
     lax.fori_loop(0, count + 2, slot_body, 0)
     for copy in new_copies(count - 1):
         copy.wait()
@@ -302,13 +329,13 @@
         in_specs=[pl.BlockSpec(memory_space=pltpu.SMEM), local, local, local] + [anywhere] * 8,
         out_specs=(anywhere, anywhere, anywhere),
         scratch_shapes=[
-            pltpu.VMEM(wqkv.shape, BF16), pltpu.VMEM(wout.shape, BF16), pltpu.VMEM(wgate.shape, BF16), pltpu.VMEM(wup.shape, BF16), pltpu.VMEM(wdown.shape, BF16),
+            pltpu.VMEM(wqkv.shape, BF16), pltpu.VMEM(wout.shape, BF16), pltpu.VMEM(wgate.shape[::-1], BF16), pltpu.VMEM(wup.shape[::-1], BF16), pltpu.VMEM(wdown.shape, BF16),
             pltpu.VMEM((batch, slots, heads, head_dim), BF16), pltpu.VMEM((batch, slots, heads, head_dim), BF16),
             pltpu.VMEM((2, batch, width), BF16), pltpu.VMEM((2, batch, width), BF16), pltpu.VMEM((3, batch, width), F32),
             pltpu.VMEM((2,) + part, BF16), pltpu.VMEM((3,) + part, BF16), pltpu.VMEM((2,) + part, BF16), pltpu.VMEM((3,) + part, BF16),
-            pltpu.VMEM((batch, width), BF16), pltpu.VMEM((batch, wgate.shape[1]), BF16), pltpu.VMEM((batch, heads * head_dim), BF16),
-            pltpu.VMEM((batch, heads, head_dim), F32), pltpu.VMEM((batch, heads, head_dim), F32), pltpu.VMEM((batch, heads, head_dim), F32), pltpu.VMEM((batch, heads, head_dim), F32),
-            pltpu.SemaphoreType.DMA((5,)), pair, pair, pair, sent, landed, sent, landed, pair, pair,
+            pltpu.VMEM((batch, width), BF16), pltpu.VMEM((batch, wdown.shape[0]), BF16), pltpu.VMEM((batch, heads * head_dim), BF16),
+            pltpu.VMEM((batch, heads, head_dim), F32), pltpu.VMEM((batch, heads, head_dim), F32), pltpu.VMEM((batch, heads, head_dim), F32), pltpu.VMEM((batch, heads, head_dim), F32), pltpu.VMEM((TILE, TILE), BF16),
+            pair, pltpu.SemaphoreType.DMA((pl.cdiv(wdown.shape[0], TILE),)), pair, pair, pair, sent, landed, sent, landed, pair, pair,
             pltpu.SemaphoreType.DMA((2, stages)), pltpu.SemaphoreType.DMA((count,)), pltpu.SemaphoreType.REGULAR,
         ],
         compiler_params=pltpu.CompilerParams(has_side_effects=True, vmem_limit_bytes=VMEM_LIMIT),
@@ -406,7 +433,7 @@
         k_rows = k_cache.reshape((rows,) + cache_shape[3:])
         v_rows = v_cache.reshape((rows,) + cache_shape[3:])
         final, knew, vnew = run_pipeline(
-            stages, lens, norm_gain[0], cos_part, sin_part, embeds.reshape(rows, width), w_qkv[0].transpose(0, 2, 1, 3).reshape(width, -1), w_out[0], w_gate[0], w_up[0], w_down[0], k_rows, v_rows)
+            stages, lens, norm_gain[0], cos_part, sin_part, embeds.reshape(rows, width), w_qkv[0].transpose(0, 2, 1, 3).reshape(width, -1), w_out[0], w_gate[0].T, w_up[0].T, w_down[0], k_rows, v_rows)
         logits, k_out, v_out = run_tail(lens, final_gain.reshape(1, width), final, knew, vnew, k_rows, v_rows, w_unembed.T)
         return logits.reshape(groups, seqs, -1), k_out.reshape(cache_shape), v_out.reshape(cache_shape)
 

time: 397 us -> 368 us (0.927)
  local copies, waits for them, and re-layouts: 44.6 us -> 12.7 us
  Pallas kernels: 348 us -> 352 us
    unnamed x6 -> x4, local copies, waits for them, and re-layouts: 44.5 us -> 12.6 us
where the time goes in v6:
time: 368 us
  Pallas kernels  352 us (96%)
  local copies, waits for them, and re-layouts  12.7 us (3%)
    pallas_call x1, Pallas kernels, run_pipeline(): pl.pallas_call(functools.partial(pipeline_kernel, stages, batch), out_sha...  304 us
    pallas_call x1, Pallas kernels, run_tail(): pl.pallas_call(tail_kernel, out_shape=(jax.ShapeDtypeStruct((rows, vocab)...  47.1 us
    unnamed x4, local copies, waits for them, and re-layouts  12.6 us

profile of v6, /device:TPU:1, one launch (start us, length us, event | category | flops | bytes accessed | tf_op | source)
XLA Modules:
  0.0 367.7 jit_solution(5315666207298960208)
XLA Ops:
  0.6 0.8 copy.15
  1.4 0.1 reshape.44.lens_ref
  1.5 0.0 copy-start
  1.5 1.4 fusion
  3.0 1.2 pad_maximum_fusion
  4.1 11.8 %copy.18 = bf16[256,8,24,128]{3,1,2,0:T(8,128)(2,1)} copy(bf16[256,8,24,128]{3,2,1,0:T(8,128)(2,1)} %bitcast.31) | data formatting | bytes 25165824
  15.9 0.0 copy-done
  16.0 304.4 %shard_map.139 = (bf16[768,2048]{1,0:T(8,128)(2,1)}, f32[768,8,128]{2,1,0:T(8,128)}, f32[768,8,128]{2,1,0:T(8,128)}) custom-call(s32[768]{0:T(1024)} %copy-done, f32[2,2048]{1,0:T(2,128)} %bitcast.37, f32[768,128]{1,0:T(8,128)} %get-tuple-element.18.cos_ref, f32[768,128]{1,0:T(8,128)} %get-tuple-element.19.sin_ref, bf16[768,2048]{1,0:T(8,128)(2,1)} %bitcast.36, ...), custom_call_target="tpu_custom_call" | custom-call | tf_op jit(solution)/shard_map/pallas_call | solution.py:326
  320.4 47.1 %shard_map.140 = (f32[768,4000]{1,0:T(8,128)}, bf16[768,16,8,128]{3,2,1,0:T(8,128)(2,1)}, bf16[768,16,8,128]{3,2,1,0:T(8,128)(2,1)}) custom-call(s32[768]{0:T(1024)} %copy-done, f32[1,2048]{1,0:T(1,128)} %bitcast.38, bf16[768,2048]{1,0:T(8,128)(2,1)} %get-tuple-element.9.final_ref, f32[768,8,128]{2,1,0:T(8,128)} %get-tuple-element.10.knew_ref, ...), custom_call_target="tpu_custom_call" | custom-call | tf_op jit(solution)/shard_map/pallas_call | solution.py:405
  (2 shorter events, 0.0 us)
Async XLA Ops:
  1.5 14.5 %copy-start = (s32[768]{0:T(1024)}, s32[768]{0:T(1024)S(1)}, u32[]{:S(2)}) copy-start(s32[768]{0:T(1024)S(1)} %reshape.44.lens_ref) | copy-start | bytes 9220
